TPU v7x, 32 devices: a whole 2x2x4 slice. The times are simulated.
32 devices in a mesh: rows: 4 (over y, x), mp: 8 (over z, core).
Axes of the slice: x: 2, y: 2, z: 4, core: 2. Of those that a mesh axis runs over, the one named last changes fastest.
Arguments:
- tokens: bfloat16 [512, 6144], P('rows', 'mp'), may hold values from -8 to 8
- norm_gain: float32 [6144], replicated, may hold values from 0.25 to 1.75
- hidden_bias: float32 [24576], P('mp'), may hold values from -3 to 3
- weight_in: bfloat16 [6144, 24576], P('rows', 'mp'), may hold values from -0.078125 to 0.078125
- weight_out: bfloat16 [24576, 6144], P('mp', 'rows'), may hold values from -0.0546875 to 0.0546875
Outputs:
- updated: bfloat16 [512, 6144], P('rows', 'mp')
All inputs are finite; a program needn't handle non-finite values.
Results may differ from a plain program's by a relative error of at most 0.0041.
Values may be sent and summed in bfloat16 or wider, within the bound.
No kernel may reach another device: no remote copies, remote signals or barrier semaphores. Data moves between devices by JAX's collectives and lax.ppermute only.
A program may use at most 128 MiB of HBM per device.

v0:
```python
import jax
import jax.numpy as jnp
from jax import lax
from jax.sharding import PartitionSpec as P


floor_value = 0.1
CORES = 2
TOKEN_CHUNKS = 2
COLUMN_CHUNKS = 2


def make_body(rows, mp):
    depth = mp // CORES
    per_row = depth // rows
    bits = [1 << n for n in range(rows.bit_length() - 1)]

    def over_rows(value, flip):
        return lax.ppermute(value, "rows", [(i, i ^ flip) for i in range(rows)])

    def over_cores(value):
        return lax.ppermute(value, "mp", [(i, i ^ 1) for i in range(mp)])

    def over_depth(value, shift):
        return lax.ppermute(value, "mp", [(i, (i + CORES * shift) % mp) for i in range(mp)])

    def spread(value, j):
        pairs = []
        for r in range(rows):
            for m in range(mp):
                z, core = divmod(m, CORES)
                target = (r * per_row + z % per_row) ^ j
                pairs.append((r * mp + m, (z // per_row) * mp + target * CORES + core))
        return lax.ppermute(value, ("rows", "mp"), pairs)

    def scatter_depth(parts):
        half = parts[0].shape[0] // 2
        middle = parts[depth // 2]
        up = down = None
        for distance in range(depth // 2, 0, -1):
            if distance == depth // 2:
                give_up, give_down = middle[:half], middle[half:]
            else:
                mine_up, mine_down = parts[depth - distance], parts[distance]
                if distance == depth // 2 - 1:
                    give_up = jnp.concatenate([mine_up[:half] + up, mine_up[half:]], axis=0)
                    give_down = jnp.concatenate([mine_down[:half], mine_down[half:] + down], axis=0)
                else:
                    give_up, give_down = mine_up + up, mine_down + down
            up = over_depth(give_up.astype(jnp.bfloat16), 1).astype(jnp.float32)
            down = over_depth(give_down.astype(jnp.bfloat16), -1).astype(jnp.float32)
        return parts[0] + up + down

    def body(tokens, norm_gain, hidden_bias, weight_in, weight_out):
        count, width = tokens.shape
        hidden_width = weight_in.shape[1]
        features = width * mp
        row, place = lax.axis_index("rows"), lax.axis_index("mp")
        core, chip = place % CORES, place // CORES

        as_float = tokens.astype(jnp.float32)
        sums = jnp.stack([jnp.sum(as_float, axis=1), jnp.sum(as_float * as_float, axis=1)])
        sums = sums + over_cores(sums)
        sums = jnp.stack([over_rows(sums, flip) if flip else sums for flip in range(rows)])
        sums = sum([over_depth(sums, shift) for shift in range(1, depth)], sums)
        row_mean = sums[:, 0] / features
        row_var = jnp.maximum(sums[:, 1] / features - row_mean * row_mean, 0.0)
        inverse = lax.rsqrt(row_var + floor_value)

        gains = lax.dynamic_slice_in_dim(norm_gain, row * (features // rows), features // rows).reshape(per_row, CORES, width)
        gains = lax.dynamic_index_in_dim(gains, core, 1, keepdims=False)

        got = []
        for j in range(depth):
            got.append(spread(tokens, j))
        stacked = jnp.stack(got)
        pieces = []
        for flip in range(rows):
            parts = []
            for sub in range(per_row):
                at = ((row ^ flip) * per_row + sub) ^ chip
                raw = lax.dynamic_index_in_dim(stacked, at, 0, keepdims=False).astype(jnp.float32)
                scaled = (raw - row_mean[flip][:, None]) * inverse[flip][:, None] * gains[sub][None, :]
                parts.append(scaled.astype(jnp.bfloat16))
            pieces.append(parts)
        x_own = [jnp.concatenate([p[sub] for p in pieces], axis=0) for sub in range(per_row)]
        x_own = x_own[0] if per_row == 1 else jnp.concatenate(x_own, axis=1)
        x_other = over_cores(x_own)
        first = core == 0
        columns = []
        for sub in range(per_row):
            at = slice(sub * width, (sub + 1) * width)
            columns.append(jnp.where(first, x_own[:, at], x_other[:, at]))
            columns.append(jnp.where(first, x_other[:, at], x_own[:, at]))
        x_all = jnp.concatenate(columns, axis=1).reshape(rows, count, features // rows)

        rows_here = count // TOKEN_CHUNKS
        cols_here = hidden_width // COLUMN_CHUNKS
        results = []
        for t in range(TOKEN_CHUNKS):
            span = slice(t * rows_here, (t + 1) * rows_here)
            x_here = x_all[:, span].reshape(rows * rows_here, features // rows)
            terms = 0.0
            for c in range(COLUMN_CHUNKS):
                cols = slice(c * cols_here, (c + 1) * cols_here)
                order = bits[c % len(bits):] + bits[: c % len(bits)]
                part = jnp.dot(x_here, weight_in[:, cols], preferred_element_type=jnp.float32)
                held = {b: part[b * rows_here : (b + 1) * rows_here] for b in range(rows)}
                for bit in order:
                    going = [b for b in held if b & bit]
                    sent = over_rows(jnp.concatenate([held[b].astype(jnp.bfloat16) for b in going], axis=0), bit)
                    held = {
                        b ^ bit: held[b ^ bit] + sent[n * rows_here : (n + 1) * rows_here].astype(jnp.float32)
                        for n, b in enumerate(going)
                    }
                hidden = jax.nn.gelu(held[0] + hidden_bias[None, cols], approximate=False).astype(jnp.bfloat16)
                names, block = [0], hidden
                for bit in reversed(order):
                    names = names + [b ^ bit for b in names]
                    block = jnp.concatenate([block, over_rows(block, bit)], axis=0)
                places = {b: n for n, b in enumerate(names)}
                if names != sorted(names):
                    block = jnp.concatenate([block[places[b] * rows_here : (places[b] + 1) * rows_here] for b in range(rows)], axis=0)
                terms = terms + jnp.dot(block, weight_out[cols], preferred_element_type=jnp.float32)

            terms = [terms[:, n * width : (n + 1) * width] for n in range(per_row * CORES)]
            lower = terms[0::CORES][0] if per_row == 1 else jnp.concatenate(terms[0::CORES], axis=1)
            upper = terms[1::CORES][0] if per_row == 1 else jnp.concatenate(terms[1::CORES], axis=1)
            given = jnp.where(first, upper, lower).astype(jnp.bfloat16)
            total = jnp.where(first, lower, upper) + over_cores(given).astype(jnp.float32)
            backs = []
            for flip in range(rows):
                piece = total[flip * rows_here : (flip + 1) * rows_here].astype(jnp.bfloat16)
                backs.append(over_rows(piece, flip) if flip else piece)
            blocks = jnp.stack(backs).reshape(rows, rows_here, per_row, width)
            blocks = jnp.moveaxis(blocks, 2, 1).reshape(depth, rows_here, width)
            parts = []
            for j in range(depth):
                target = (chip - j) % depth
                index = ((target // per_row) ^ row) * per_row + target % per_row
                parts.append(lax.dynamic_index_in_dim(blocks, index, 0, keepdims=False).astype(jnp.float32))
            results.append((as_float[span] + scatter_depth(parts)).astype(jnp.bfloat16))
        return results[0] if TOKEN_CHUNKS == 1 else jnp.concatenate(results, axis=0)

    return body


def solution(mesh):
    rows, mp = mesh.shape["rows"], mesh.shape["mp"]
    inner = make_body(rows, mp)

    return jax.shard_map(
        inner,
        mesh=mesh,
        in_specs=(P("rows", "mp"), P(), P("mp"), P("rows", "mp"), P("mp", "rows")),
        out_specs=P("rows", "mp"),
        check_vma=False,
    )
```

profile of v0, /device:TPU:0, one launch (start us, length us, event | category | flops | bytes accessed | tf_op | source)
XLA Modules:
  0.0 144.6 jit_solution(5295052334157210227)
XLA Ops:
  0.0 1.1 convert_reduce_fusion
  1.1 0.6 collective-permute-start.4
  1.6 0.8 collective-permute-done.4
  2.5 3.8 %collective-permute-start.7 = (f32[2,128]{1,0:T(2,128)S(1)}, f32[2,128]{1,0:T(2,128)S(1)}, u32[]{:S(2)}, u32[]{:S(2)}) collective-permute-start(f32[2,128]{1,0:T(2,128)S(1)} %fusion.124), channel_id=1, source_target_pairs={{0,24},{8,16},{16,8},{24,0},{1,25},{9,17},{17,9},{25,1},{2,26},{10... | collective-permute-start | bytes 3080 | tf_op jit(solution)/shard_map/ppermute | solution.py:19
  6.3 0.5 collective-permute-start.5
  7.0 0.9 collective-permute-done.7
  7.9 2.0 %collective-permute-done.5 = f32[2,128]{1,0:T(2,128)S(1)} collective-permute-done((f32[2,128]{1,0:T(2,128)S(1)}, f32[2,128]{1,0:T(2,128)S(1)}, u32[]{:S(2)}, u32[]{:S(2)}) %collective-permute-start.5) | collective-permute-done | bytes 1056 | tf_op jit(solution)/shard_map/ppermute | solution.py:19
  9.9 0.5 collective-permute-done.6
  10.4 3.6 %collective-permute-start.10 = (f32[4,2,128]{2,1,0:T(2,128)S(1)}, f32[4,2,128]{2,1,0:T(2,128)S(1)}, u32[]{:S(2)}, u32[]{:S(2)}) collective-permute-start(f32[4,2,128]{2,1,0:T(2,128)S(1)} %pad_maximum_fusion.16), channel_id=1, source_target_pairs={{0,6},{1,7},{2,0},{3,1},{4,2},{5,3},{6,4},{7,5},{8,14},{9,15},{10,... | collective-permute-start | bytes 12296 | tf_op jit(solution)/shard_map/ppermute | solution.py:25
  14.0 1.0 collective-permute-start.9
  15.0 1.6 %collective-permute-start = (bf16[128,768]{1,0:T(8,128)(2,1)}, bf16[128,768]{1,0:T(8,128)(2,1)S(1)}, u32[]{:S(2)}, u32[]{:S(2)}) collective-permute-start(bf16[128,768]{1,0:T(8,128)(2,1)} %param.5), channel_id=1, source_target_pairs={{0,0},{1,1},{2,8},{3,9},{4,16},{5,17},{6,24},{7,25},{8,2},{9,3},{1... | collective-permute-start | bytes 589832 | tf_op jit(solution)/shard_map/ppermute | solution.py:34
  16.6 3.8 %collective-permute-start.1 = (bf16[128,768]{1,0:T(8,128)(2,1)}, bf16[128,768]{1,0:T(8,128)(2,1)S(1)}, u32[]{:S(2)}, u32[]{:S(2)}) collective-permute-start(bf16[128,768]{1,0:T(8,128)(2,1)} %param.5), channel_id=1, source_target_pairs={{0,2},{1,3},{2,10},{3,11},{4,18},{5,19},{6,26},{7,27},{8,0},{9,1},... | collective-permute-start | bytes 589832 | tf_op jit(solution)/shard_map/ppermute | solution.py:34
  20.4 0.8 dynamic_slice.46
  21.2 2.4 %collective-permute-start.2 = (bf16[128,768]{1,0:T(8,128)(2,1)}, bf16[128,768]{1,0:T(8,128)(2,1)S(1)}, u32[]{:S(2)}, u32[]{:S(2)}) collective-permute-start(bf16[128,768]{1,0:T(8,128)(2,1)} %param.5), channel_id=1, source_target_pairs={{0,4},{1,5},{2,12},{3,13},{4,20},{5,21},{6,28},{7,29},{8,6},{9,7},... | collective-permute-start | bytes 589832 | tf_op jit(solution)/shard_map/ppermute | solution.py:34
  23.6 1.9 %collective-permute-start.3 = (bf16[128,768]{1,0:T(8,128)(2,1)}, bf16[128,768]{1,0:T(8,128)(2,1)S(1)}, u32[]{:S(2)}, u32[]{:S(2)}) collective-permute-start(bf16[128,768]{1,0:T(8,128)(2,1)} %param.5), channel_id=1, source_target_pairs={{0,6},{1,7},{2,14},{3,15},{4,22},{5,23},{6,30},{7,31},{8,4},{9,5},... | collective-permute-start | bytes 589832 | tf_op jit(solution)/shard_map/ppermute | solution.py:34
  25.6 0.4 collective-permute-done.1
  26.0 4.9 %collective-permute-done.2 = bf16[128,768]{1,0:T(8,128)(2,1)S(1)} collective-permute-done((bf16[128,768]{1,0:T(8,128)(2,1)}, bf16[128,768]{1,0:T(8,128)(2,1)S(1)}, u32[]{:S(2)}, u32[]{:S(2)}) %collective-permute-start.2) | collective-permute-done | bytes 196640 | tf_op jit(solution)/shard_map/ppermute | solution.py:34
  30.9 1.2 collective-permute-done.3
  32.2 0.3 fusion.81
  32.9 2.0 %collective-permute-done.11 = bf16[512,768]{1,0:T(8,128)(2,1)S(1)} collective-permute-done((bf16[512,768]{1,0:T(8,128)(2,1)S(1)}, bf16[512,768]{1,0:T(8,128)(2,1)S(1)}, u32[]{:S(2)}, u32[]{:S(2)}) %collective-permute-start.11) | collective-permute-done | bytes 786464 | tf_op jit(solution)/shard_map/ppermute | solution.py:22
  35.5 3.2 %copy-done.2 = bf16[1536,3072]{1,0:T(8,128)(2,1)S(1)} copy-done((bf16[1536,3072]{1,0:T(8,128)(2,1)S(1)}, bf16[1536,3072]{1,0:T(8,128)(2,1)}, u32[]{:S(2)}) %copy-start.2) | copy-done | bytes 9437208
  38.6 1.4 fusion.132
  40.0 1.4 fusion.4
  41.5 4.5 %collective-permute-start.28 = (bf16[128,1536]{1,0:T(8,128)(2,1)S(1)}, bf16[128,1536]{1,0:T(8,128)(2,1)S(1)}, u32[]{:S(2)}, u32[]{:S(2)}) collective-permute-start(bf16[128,1536]{1,0:T(8,128)(2,1)S(1)} %pad_maximum_fusion.7), channel_id=1, source_target_pairs={{0,8},{8,0},{16,24},{24,16},{1,9},{9,1},{17,25},{25,17},{2,10},{10... | collective-permute-start | bytes 1179656 | tf_op jit(solution)/shard_map/ppermute | solution.py:19
  46.0 1.4 fusion.131
  47.6 9.0 %collective-permute-start.32 = (bf16[128,1536]{1,0:T(8,128)(2,1)S(1)}, bf16[128,1536]{1,0:T(8,128)(2,1)S(1)}, u32[]{:S(2)}, u32[]{:S(2)}) collective-permute-start(bf16[128,1536]{1,0:T(8,128)(2,1)S(1)} %slice.538), channel_id=1, source_target_pairs={{0,16},{8,24},{16,0},{24,8},{1,17},{9,25},{17,1},{25,9},{2,18},{10... | collective-permute-start | bytes 1179656 | tf_op jit(solution)/shard_map/ppermute | solution.py:19
  56.5 1.4 fusion.6
  58.1 6.8 %collective-permute-start.29 = (bf16[64,1536]{1,0:T(8,128)(2,1)S(1)}, bf16[64,1536]{1,0:T(8,128)(2,1)S(1)}, u32[]{:S(2)}, u32[]{:S(2)}) collective-permute-start(bf16[64,1536]{1,0:T(8,128)(2,1)S(1)} %fusion.61), channel_id=1, source_target_pairs={{0,16},{8,24},{16,0},{24,8},{1,17},{9,25},{17,1},{25,9},{2,18},{10... | collective-permute-start | bytes 589832 | tf_op jit(solution)/shard_map/ppermute | solution.py:19
  65.0 7.6 %collective-permute-start.13 = (bf16[64,1536]{1,0:T(8,128)(2,1)S(1)}, bf16[64,1536]{1,0:T(8,128)(2,1)S(1)}, u32[]{:S(2)}, u32[]{:S(2)}) collective-permute-start(bf16[64,1536]{1,0:T(8,128)(2,1)S(1)} %fusion.67), channel_id=1, source_target_pairs={{0,16},{8,24},{16,0},{24,8},{1,17},{9,25},{17,1},{25,9},{2,18},{10... | collective-permute-start | bytes 589832 | tf_op jit(solution)/shard_map/ppermute | solution.py:19
  72.6 0.4 collective-permute-start.33
  73.0 2.0 %collective-permute-done.16 = bf16[128,1536]{1,0:T(8,128)(2,1)S(1)} collective-permute-done((bf16[128,1536]{1,0:T(8,128)(2,1)S(1)}, bf16[128,1536]{1,0:T(8,128)(2,1)S(1)}, u32[]{:S(2)}, u32[]{:S(2)}) %collective-permute-start.16) | collective-permute-done | bytes 393248 | tf_op jit(solution)/shard_map/ppermute | solution.py:19
  75.1 4.1 %collective-permute-done.29 = bf16[64,1536]{1,0:T(8,128)(2,1)S(1)} collective-permute-done((bf16[64,1536]{1,0:T(8,128)(2,1)S(1)}, bf16[64,1536]{1,0:T(8,128)(2,1)S(1)}, u32[]{:S(2)}, u32[]{:S(2)}) %collective-permute-start.29) | collective-permute-done | bytes 196640 | tf_op jit(solution)/shard_map/ppermute | solution.py:19
  79.1 3.1 %collective-permute-done.13 = bf16[64,1536]{1,0:T(8,128)(2,1)S(1)} collective-permute-done((bf16[64,1536]{1,0:T(8,128)(2,1)S(1)}, bf16[64,1536]{1,0:T(8,128)(2,1)S(1)}, u32[]{:S(2)}, u32[]{:S(2)}) %collective-permute-start.13) | collective-permute-done | bytes 196640 | tf_op jit(solution)/shard_map/ppermute | solution.py:19
  82.3 1.8 %fusion.48 = (bf16[64,1536]{1,0:T(8,128)(2,1)S(1)}, bf16[64,1536]{1,0:T(8,128)(2,1)S(1)}) fusion(bf16[64,1536]{1,0:T(8,128)(2,1)S(1)} %collective-permute-done.13, f32[256,1536]{1,0:T(8,128)S(1)} %get-tuple-element.62, bf16[128,1536]{1,0:T(8,128)(2,1)S(1)} %collective-permute-done.12, f32[1536]{0:T(1024)S(1)} %get-tuple-element.45, ...), kind=kLoop, calls=%fused_computation.59 | loop fusion | flops 13762560 | bytes 1972224 | tf_op jit(solution)/shard_map/convert_element_type | solution.py:116
  84.1 1.8 %collective-permute-start.30 = (bf16[64,1536]{1,0:T(8,128)(2,1)S(1)}, bf16[64,1536]{1,0:T(8,128)(2,1)S(1)}, u32[]{:S(2)}, u32[]{:S(2)}) collective-permute-start(bf16[64,1536]{1,0:T(8,128)(2,1)S(1)} %get-tuple-element.48), channel_id=1, source_target_pairs={{0,16},{8,24},{16,0},{24,8},{1,17},{9,25},{17,1},{25,9},{2,18},{10... | collective-permute-start | bytes 589832 | tf_op jit(solution)/shard_map/ppermute | solution.py:19
  85.9 1.8 %fusion.51 = (bf16[64,1536]{1,0:T(8,128)(2,1)S(1)}, bf16[64,1536]{1,0:T(8,128)(2,1)S(1)}) fusion(bf16[64,1536]{1,0:T(8,128)(2,1)S(1)} %collective-permute-done.17, f32[256,1536]{1,0:T(8,128)S(1)} %fusion.6, bf16[128,1536]{1,0:T(8,128)(2,1)S(1)} %collective-permute-done.16, f32[1536]{0:T(1024)S(1)} %get-tuple-element.46, ...), kind=kLoop, calls=%fused_computation.62 | loop fusion | flops 13762560 | bytes 1972224 | tf_op jit(solution)/shard_map/convert_element_type | solution.py:116
  87.7 0.4 collective-permute-start.34
  88.3 1.7 %collective-permute-start.18 = (bf16[64,1536]{1,0:T(8,128)(2,1)S(1)}, bf16[64,1536]{1,0:T(8,128)(2,1)S(1)}, u32[]{:S(2)}, u32[]{:S(2)}) collective-permute-start(bf16[64,1536]{1,0:T(8,128)(2,1)S(1)} %get-tuple-element.49), channel_id=1, source_target_pairs={{0,8},{8,0},{16,24},{24,16},{1,9},{9,1},{17,25},{25,17},{2,10},{10... | collective-permute-start | bytes 589832 | tf_op jit(solution)/shard_map/ppermute | solution.py:19
  90.1 0.9 collective-permute-done.30
  91.0 4.5 %collective-permute-done.34 = bf16[64,1536]{1,0:T(8,128)(2,1)S(1)} collective-permute-done((bf16[64,1536]{1,0:T(8,128)(2,1)S(1)}, bf16[64,1536]{1,0:T(8,128)(2,1)S(1)}, u32[]{:S(2)}, u32[]{:S(2)}) %collective-permute-start.34) | collective-permute-done | bytes 196640 | tf_op jit(solution)/shard_map/ppermute | solution.py:19
  95.6 0.4 collective-permute-start.35
  95.9 1.1 collective-permute-start.15
  97.0 2.7 %collective-permute-done.18 = bf16[64,1536]{1,0:T(8,128)(2,1)S(1)} collective-permute-done((bf16[64,1536]{1,0:T(8,128)(2,1)S(1)}, bf16[64,1536]{1,0:T(8,128)(2,1)S(1)}, u32[]{:S(2)}, u32[]{:S(2)}) %collective-permute-start.18) | collective-permute-done | bytes 196640 | tf_op jit(solution)/shard_map/ppermute | solution.py:19
  99.8 0.4 collective-permute-start.19
  100.1 8.0 %collective-permute-done.31 = bf16[128,1536]{1,0:T(8,128)(2,1)S(1)} collective-permute-done((bf16[128,1536]{1,0:T(8,128)(2,1)S(1)}, bf16[128,1536]{1,0:T(8,128)(2,1)S(1)}, u32[]{:S(2)}, u32[]{:S(2)}) %collective-permute-start.31) | collective-permute-done | bytes 393248 | tf_op jit(solution)/shard_map/ppermute | solution.py:19
  108.2 1.4 fusion
  109.6 1.6 %fusion.19 = f32[256,1536]{1,0:T(8,128)S(1)} fusion(f32[256,1536]{1,0:T(8,128)S(1)} %fusion, bf16[3072,1536]{1,0:T(8,128)(2,1)S(1)} %bitcast.126, bf16[64,1536]{1,0:T(8,128)(2,1)S(1)} %get-tuple-element.44, bf16[64,1536]{1,0:T(8,128)(2,1)S(1)} %collective-permute-done.30, bf16[64,1536]{1,0:T(8,128)(2,1)S(1)} %get-tuple-element.43, ...), kind=kOutput, calls=%fused_computation.17 | convolution fusion | flops 1211498496 | bytes 8650752 | tf_op jit(solution)/shard_map/dot_general | solution.py:124
  111.4 2.7 %collective-permute-done.15 = bf16[128,1536]{1,0:T(8,128)(2,1)S(1)} collective-permute-done((bf16[128,1536]{1,0:T(8,128)(2,1)S(1)}, bf16[128,1536]{1,0:T(8,128)(2,1)S(1)}, u32[]{:S(2)}, u32[]{:S(2)}) %collective-permute-start.15) | collective-permute-done | bytes 393248 | tf_op jit(solution)/shard_map/ppermute | solution.py:19
  114.1 1.4 fusion.2
  115.5 1.4 fusion.16
  117.2 0.6 collective-permute-start.37
  117.9 0.6 collective-permute-start.38
  118.4 2.3 %collective-permute-start.39 = (bf16[64,768]{1,0:T(8,128)(2,1)S(1)}, bf16[64,768]{1,0:T(8,128)(2,1)S(1)}, u32[]{:S(2)}, u32[]{:S(2)}) collective-permute-start(bf16[64,768]{1,0:T(8,128)(2,1)S(1)} %get-tuple-element.40), channel_id=1, source_target_pairs={{0,24},{8,16},{16,8},{24,0},{1,25},{9,17},{17,9},{25,1},{2,26},{10... | collective-permute-start | bytes 294920 | tf_op jit(solution)/shard_map/ppermute | solution.py:19
  121.0 0.6 collective-permute-start.21
  121.6 0.6 collective-permute-start.22
  122.2 0.8 collective-permute-done.37
  122.9 1.6 %collective-permute-start.23 = (bf16[64,768]{1,0:T(8,128)(2,1)S(1)}, bf16[64,768]{1,0:T(8,128)(2,1)S(1)}, u32[]{:S(2)}, u32[]{:S(2)}) collective-permute-start(bf16[64,768]{1,0:T(8,128)(2,1)S(1)} %get-tuple-element.28), channel_id=1, source_target_pairs={{0,24},{8,16},{16,8},{24,0},{1,25},{9,17},{17,9},{25,1},{2,26},{10... | collective-permute-start | bytes 294920 | tf_op jit(solution)/shard_map/ppermute | solution.py:19
  124.5 0.5 collective-permute-done.38
  125.3 3.8 %collective-permute-start.42 = (bf16[32,768]{1,0:T(8,128)(2,1)S(1)}, bf16[32,768]{1,0:T(8,128)(2,1)S(1)}, u32[]{:S(2)}, u32[]{:S(2)}) collective-permute-start(bf16[32,768]{1,0:T(8,128)(2,1)S(1)} %get-tuple-element.37), channel_id=1, source_target_pairs={{0,6},{1,7},{2,0},{3,1},{4,2},{5,3},{6,4},{7,5},{8,14},{9,15},{10,... | collective-permute-start | bytes 147464 | tf_op jit(solution)/shard_map/ppermute | solution.py:25
  129.3 3.8 %collective-permute-start.26 = (bf16[32,768]{1,0:T(8,128)(2,1)S(1)}, bf16[32,768]{1,0:T(8,128)(2,1)S(1)}, u32[]{:S(2)}, u32[]{:S(2)}) collective-permute-start(bf16[32,768]{1,0:T(8,128)(2,1)S(1)} %get-tuple-element.25), channel_id=1, source_target_pairs={{0,6},{1,7},{2,0},{3,1},{4,2},{5,3},{6,4},{7,5},{8,14},{9,15},{10,... | collective-permute-start | bytes 147464 | tf_op jit(solution)/shard_map/ppermute | solution.py:25
  133.2 3.8 %collective-permute-start.43 = (bf16[64,768]{1,0:T(8,128)(2,1)S(1)}, bf16[64,768]{1,0:T(8,128)(2,1)S(1)}, u32[]{:S(2)}, u32[]{:S(2)}) collective-permute-start(bf16[64,768]{1,0:T(8,128)(2,1)S(1)} %pad_maximum_fusion.15), channel_id=1, source_target_pairs={{0,6},{1,7},{2,0},{3,1},{4,2},{5,3},{6,4},{7,5},{8,14},{9,15},{10,... | collective-permute-start | bytes 294920 | tf_op jit(solution)/shard_map/ppermute | solution.py:25
  137.2 3.8 %collective-permute-start.27 = (bf16[64,768]{1,0:T(8,128)(2,1)S(1)}, bf16[64,768]{1,0:T(8,128)(2,1)S(1)}, u32[]{:S(2)}, u32[]{:S(2)}) collective-permute-start(bf16[64,768]{1,0:T(8,128)(2,1)S(1)} %pad_maximum_fusion.13), channel_id=1, source_target_pairs={{0,6},{1,7},{2,0},{3,1},{4,2},{5,3},{6,4},{7,5},{8,14},{9,15},{10,... | collective-permute-start | bytes 294920 | tf_op jit(solution)/shard_map/ppermute | solution.py:25
  141.1 2.7 %collective-permute-done.25 = bf16[64,768]{1,0:T(8,128)(2,1)S(1)} collective-permute-done((bf16[64,768]{1,0:T(8,128)(2,1)S(1)}, bf16[64,768]{1,0:T(8,128)(2,1)S(1)}, u32[]{:S(2)}, u32[]{:S(2)}) %collective-permute-start.25) | collective-permute-done | bytes 98336 | tf_op jit(solution)/shard_map/ppermute | solution.py:25
  143.9 0.7 pad_maximum_fusion.11
  (100 shorter events, 3.6 us)
Async XLA Ops:
  1.1 1.4 collective-permute-start.4
  2.5 5.4 %collective-permute-start.7 = (f32[2,128]{1,0:T(2,128)S(1)}, f32[2,128]{1,0:T(2,128)S(1)}, u32[]{:S(2)}, u32[]{:S(2)}) collective-permute-start(f32[2,128]{1,0:T(2,128)S(1)} %fusion.124), channel_id=1, source_target_pairs={{0,24},{8,16},{16,8},{24,0},{1,25},{9,17},{17,9},{25,1},{2,26},{10... | collective-permute-start | bytes 3080 | tf_op jit(solution)/shard_map/ppermute | solution.py:19
  6.3 3.6 %collective-permute-start.5 = (f32[2,128]{1,0:T(2,128)S(1)}, f32[2,128]{1,0:T(2,128)S(1)}, u32[]{:S(2)}, u32[]{:S(2)}) collective-permute-start(f32[2,128]{1,0:T(2,128)S(1)} %fusion.124), channel_id=1, source_target_pairs={{0,8},{8,0},{16,24},{24,16},{1,9},{9,1},{17,25},{25,17},{2,10},{10... | collective-permute-start | bytes 3080 | tf_op jit(solution)/shard_map/ppermute | solution.py:19
  6.8 3.6 %collective-permute-start.6 = (f32[2,128]{1,0:T(2,128)S(1)}, f32[2,128]{1,0:T(2,128)S(1)}, u32[]{:S(2)}, u32[]{:S(2)}) collective-permute-start(f32[2,128]{1,0:T(2,128)S(1)} %fusion.124), channel_id=1, source_target_pairs={{0,16},{8,24},{16,0},{24,8},{1,17},{9,25},{17,1},{25,9},{2,18},{10... | collective-permute-start | bytes 3080 | tf_op jit(solution)/shard_map/ppermute | solution.py:19
  10.4 10.8 %collective-permute-start.10 = (f32[4,2,128]{2,1,0:T(2,128)S(1)}, f32[4,2,128]{2,1,0:T(2,128)S(1)}, u32[]{:S(2)}, u32[]{:S(2)}) collective-permute-start(f32[4,2,128]{2,1,0:T(2,128)S(1)} %pad_maximum_fusion.16), channel_id=1, source_target_pairs={{0,6},{1,7},{2,0},{3,1},{4,2},{5,3},{6,4},{7,5},{8,14},{9,15},{10,... | collective-permute-start | bytes 12296 | tf_op jit(solution)/shard_map/ppermute | solution.py:25
  14.0 9.6 %collective-permute-start.8 = (f32[4,2,128]{2,1,0:T(2,128)S(1)}, f32[4,2,128]{2,1,0:T(2,128)S(1)}, u32[]{:S(2)}, u32[]{:S(2)}) collective-permute-start(f32[4,2,128]{2,1,0:T(2,128)S(1)} %pad_maximum_fusion.16), channel_id=1, source_target_pairs={{0,2},{1,3},{2,4},{3,5},{4,6},{5,7},{6,0},{7,1},{8,10},{9,11},{10,... | collective-permute-start | bytes 12296 | tf_op jit(solution)/shard_map/ppermute | solution.py:25
  14.0 11.5 %collective-permute-start.9 = (f32[4,2,128]{2,1,0:T(2,128)S(1)}, f32[4,2,128]{2,1,0:T(2,128)S(1)}, u32[]{:S(2)}, u32[]{:S(2)}) collective-permute-start(f32[4,2,128]{2,1,0:T(2,128)S(1)} %pad_maximum_fusion.16), channel_id=1, source_target_pairs={{0,4},{1,5},{2,6},{3,7},{4,0},{5,1},{6,2},{7,3},{8,12},{9,13},{10,... | collective-permute-start | bytes 12296 | tf_op jit(solution)/shard_map/ppermute | solution.py:25
  15.0 10.5 %collective-permute-start = (bf16[128,768]{1,0:T(8,128)(2,1)}, bf16[128,768]{1,0:T(8,128)(2,1)S(1)}, u32[]{:S(2)}, u32[]{:S(2)}) collective-permute-start(bf16[128,768]{1,0:T(8,128)(2,1)} %param.5), channel_id=1, source_target_pairs={{0,0},{1,1},{2,8},{3,9},{4,16},{5,17},{6,24},{7,25},{8,2},{9,3},{1... | collective-permute-start | bytes 589832 | tf_op jit(solution)/shard_map/ppermute | solution.py:34
  16.6 9.4 %collective-permute-start.1 = (bf16[128,768]{1,0:T(8,128)(2,1)}, bf16[128,768]{1,0:T(8,128)(2,1)S(1)}, u32[]{:S(2)}, u32[]{:S(2)}) collective-permute-start(bf16[128,768]{1,0:T(8,128)(2,1)} %param.5), channel_id=1, source_target_pairs={{0,2},{1,3},{2,10},{3,11},{4,18},{5,19},{6,26},{7,27},{8,0},{9,1},... | collective-permute-start | bytes 589832 | tf_op jit(solution)/shard_map/ppermute | solution.py:34
  21.2 9.7 %collective-permute-start.2 = (bf16[128,768]{1,0:T(8,128)(2,1)}, bf16[128,768]{1,0:T(8,128)(2,1)S(1)}, u32[]{:S(2)}, u32[]{:S(2)}) collective-permute-start(bf16[128,768]{1,0:T(8,128)(2,1)} %param.5), channel_id=1, source_target_pairs={{0,4},{1,5},{2,12},{3,13},{4,20},{5,21},{6,28},{7,29},{8,6},{9,7},... | collective-permute-start | bytes 589832 | tf_op jit(solution)/shard_map/ppermute | solution.py:34
  23.6 8.5 %collective-permute-start.3 = (bf16[128,768]{1,0:T(8,128)(2,1)}, bf16[128,768]{1,0:T(8,128)(2,1)S(1)}, u32[]{:S(2)}, u32[]{:S(2)}) collective-permute-start(bf16[128,768]{1,0:T(8,128)(2,1)} %param.5), channel_id=1, source_target_pairs={{0,6},{1,7},{2,14},{3,15},{4,22},{5,23},{6,30},{7,31},{8,4},{9,5},... | collective-permute-start | bytes 589832 | tf_op jit(solution)/shard_map/ppermute | solution.py:34
  32.2 0.7 copy-start.1
  32.6 2.4 %collective-permute-start.11 = (bf16[512,768]{1,0:T(8,128)(2,1)S(1)}, bf16[512,768]{1,0:T(8,128)(2,1)S(1)}, u32[]{:S(2)}, u32[]{:S(2)}) collective-permute-start(bf16[512,768]{1,0:T(8,128)(2,1)S(1)} %pad_maximum_fusion.2), channel_id=1, source_target_pairs={{0,1},{1,0},{2,3},{3,2},{4,5},{5,4},{6,7},{7,6},{8,9},{9,8},{10,11... | collective-permute-start | bytes 2359304 | tf_op jit(solution)/shard_map/ppermute | solution.py:22
  34.9 3.7 %copy-start.2 = (bf16[1536,3072]{1,0:T(8,128)(2,1)S(1)}, bf16[1536,3072]{1,0:T(8,128)(2,1)}, u32[]{:S(2)}) copy-start(bf16[1536,3072]{1,0:T(8,128)(2,1)} %param.8) | copy-start | bytes 28311556
  41.5 16.6 %collective-permute-start.28 = (bf16[128,1536]{1,0:T(8,128)(2,1)S(1)}, bf16[128,1536]{1,0:T(8,128)(2,1)S(1)}, u32[]{:S(2)}, u32[]{:S(2)}) collective-permute-start(bf16[128,1536]{1,0:T(8,128)(2,1)S(1)} %pad_maximum_fusion.7), channel_id=1, source_target_pairs={{0,8},{8,0},{16,24},{24,16},{1,9},{9,1},{17,25},{25,17},{2,10},{10... | collective-permute-start | bytes 1179656 | tf_op jit(solution)/shard_map/ppermute | solution.py:19
  47.4 17.5 %collective-permute-start.12 = (bf16[128,1536]{1,0:T(8,128)(2,1)S(1)}, bf16[128,1536]{1,0:T(8,128)(2,1)S(1)}, u32[]{:S(2)}, u32[]{:S(2)}) collective-permute-start(bf16[128,1536]{1,0:T(8,128)(2,1)S(1)} %pad_maximum_fusion.3), channel_id=1, source_target_pairs={{0,8},{8,0},{16,24},{24,16},{1,9},{9,1},{17,25},{25,17},{2,10},{10... | collective-permute-start | bytes 1179656 | tf_op jit(solution)/shard_map/ppermute | solution.py:19
  47.6 25.0 %collective-permute-start.32 = (bf16[128,1536]{1,0:T(8,128)(2,1)S(1)}, bf16[128,1536]{1,0:T(8,128)(2,1)S(1)}, u32[]{:S(2)}, u32[]{:S(2)}) collective-permute-start(bf16[128,1536]{1,0:T(8,128)(2,1)S(1)} %slice.538), channel_id=1, source_target_pairs={{0,16},{8,24},{16,0},{24,8},{1,17},{9,25},{17,1},{25,9},{2,18},{10... | collective-permute-start | bytes 1179656 | tf_op jit(solution)/shard_map/ppermute | solution.py:19
  56.5 51.7 %slice-start = ((s8[9437184]{0:T(1024)(128)(4,1)}), s8[1048576]{0:T(1024)(128)(4,1)S(1)}, s32[]{:S(2)}) async-start(s8[9437184]{0:T(1024)(128)(4,1)} %bitcast.125), calls=%async_computation | async-start | bytes 2097152
  56.5 51.7 %slice-start.1 = ((s8[9437184]{0:T(1024)(128)(4,1)}), s8[4194304]{0:T(1024)(128)(4,1)S(1)}, s32[]{:S(2)}) async-start(s8[9437184]{0:T(1024)(128)(4,1)} %bitcast.125), calls=%async_computation.1 | async-start | bytes 8388608
  58.0 17.0 %collective-permute-start.16 = (bf16[128,1536]{1,0:T(8,128)(2,1)S(1)}, bf16[128,1536]{1,0:T(8,128)(2,1)S(1)}, u32[]{:S(2)}, u32[]{:S(2)}) collective-permute-start(bf16[128,1536]{1,0:T(8,128)(2,1)S(1)} %slice.539), channel_id=1, source_target_pairs={{0,16},{8,24},{16,0},{24,8},{1,17},{9,25},{17,1},{25,9},{2,18},{10... | collective-permute-start | bytes 1179656 | tf_op jit(solution)/shard_map/ppermute | solution.py:19
  58.1 21.0 %collective-permute-start.29 = (bf16[64,1536]{1,0:T(8,128)(2,1)S(1)}, bf16[64,1536]{1,0:T(8,128)(2,1)S(1)}, u32[]{:S(2)}, u32[]{:S(2)}) collective-permute-start(bf16[64,1536]{1,0:T(8,128)(2,1)S(1)} %fusion.61), channel_id=1, source_target_pairs={{0,16},{8,24},{16,0},{24,8},{1,17},{9,25},{17,1},{25,9},{2,18},{10... | collective-permute-start | bytes 589832 | tf_op jit(solution)/shard_map/ppermute | solution.py:19
  65.0 17.2 %collective-permute-start.13 = (bf16[64,1536]{1,0:T(8,128)(2,1)S(1)}, bf16[64,1536]{1,0:T(8,128)(2,1)S(1)}, u32[]{:S(2)}, u32[]{:S(2)}) collective-permute-start(bf16[64,1536]{1,0:T(8,128)(2,1)S(1)} %fusion.67), channel_id=1, source_target_pairs={{0,16},{8,24},{16,0},{24,8},{1,17},{9,25},{17,1},{25,9},{2,18},{10... | collective-permute-start | bytes 589832 | tf_op jit(solution)/shard_map/ppermute | solution.py:19
  72.6 13.3 %collective-permute-start.33 = (bf16[64,1536]{1,0:T(8,128)(2,1)S(1)}, bf16[64,1536]{1,0:T(8,128)(2,1)S(1)}, u32[]{:S(2)}, u32[]{:S(2)}) collective-permute-start(bf16[64,1536]{1,0:T(8,128)(2,1)S(1)} %fusion.58), channel_id=1, source_target_pairs={{0,8},{8,0},{16,24},{24,16},{1,9},{9,1},{17,25},{25,17},{2,10},{10... | collective-permute-start | bytes 589832 | tf_op jit(solution)/shard_map/ppermute | solution.py:19
  75.0 10.9 %collective-permute-start.17 = (bf16[64,1536]{1,0:T(8,128)(2,1)S(1)}, bf16[64,1536]{1,0:T(8,128)(2,1)S(1)}, u32[]{:S(2)}, u32[]{:S(2)}) collective-permute-start(bf16[64,1536]{1,0:T(8,128)(2,1)S(1)} %fusion.64), channel_id=1, source_target_pairs={{0,8},{8,0},{16,24},{24,16},{1,9},{9,1},{17,25},{25,17},{2,10},{10... | collective-permute-start | bytes 589832 | tf_op jit(solution)/shard_map/ppermute | solution.py:19
  82.3 26.0 %slice-start.2 = ((s8[9437184]{0:T(1024)(128)(4,1)}), s8[4194304]{0:T(1024)(128)(4,1)S(1)}, s32[]{:S(2)}) async-start(s8[9437184]{0:T(1024)(128)(4,1)} %bitcast.125), calls=%async_computation.2 | async-start | bytes 8388608
  84.1 6.9 %collective-permute-start.30 = (bf16[64,1536]{1,0:T(8,128)(2,1)S(1)}, bf16[64,1536]{1,0:T(8,128)(2,1)S(1)}, u32[]{:S(2)}, u32[]{:S(2)}) collective-permute-start(bf16[64,1536]{1,0:T(8,128)(2,1)S(1)} %get-tuple-element.48), channel_id=1, source_target_pairs={{0,16},{8,24},{16,0},{24,8},{1,17},{9,25},{17,1},{25,9},{2,18},{10... | collective-permute-start | bytes 589832 | tf_op jit(solution)/shard_map/ppermute | solution.py:19
  87.7 7.8 %collective-permute-start.34 = (bf16[64,1536]{1,0:T(8,128)(2,1)S(1)}, bf16[64,1536]{1,0:T(8,128)(2,1)S(1)}, u32[]{:S(2)}, u32[]{:S(2)}) collective-permute-start(bf16[64,1536]{1,0:T(8,128)(2,1)S(1)} %get-tuple-element.50), channel_id=1, source_target_pairs={{0,8},{8,0},{16,24},{24,16},{1,9},{9,1},{17,25},{25,17},{2,10},{10... | collective-permute-start | bytes 589832 | tf_op jit(solution)/shard_map/ppermute | solution.py:19
  88.1 7.9 %collective-permute-start.14 = (bf16[64,1536]{1,0:T(8,128)(2,1)S(1)}, bf16[64,1536]{1,0:T(8,128)(2,1)S(1)}, u32[]{:S(2)}, u32[]{:S(2)}) collective-permute-start(bf16[64,1536]{1,0:T(8,128)(2,1)S(1)} %get-tuple-element.47), channel_id=1, source_target_pairs={{0,16},{8,24},{16,0},{24,8},{1,17},{9,25},{17,1},{25,9},{2,18},{10... | collective-permute-start | bytes 589832 | tf_op jit(solution)/shard_map/ppermute | solution.py:19
  88.3 11.4 %collective-permute-start.18 = (bf16[64,1536]{1,0:T(8,128)(2,1)S(1)}, bf16[64,1536]{1,0:T(8,128)(2,1)S(1)}, u32[]{:S(2)}, u32[]{:S(2)}) collective-permute-start(bf16[64,1536]{1,0:T(8,128)(2,1)S(1)} %get-tuple-element.49), channel_id=1, source_target_pairs={{0,8},{8,0},{16,24},{24,16},{1,9},{9,1},{17,25},{25,17},{2,10},{10... | collective-permute-start | bytes 589832 | tf_op jit(solution)/shard_map/ppermute | solution.py:19
  91.0 17.2 %collective-permute-start.31 = (bf16[128,1536]{1,0:T(8,128)(2,1)S(1)}, bf16[128,1536]{1,0:T(8,128)(2,1)S(1)}, u32[]{:S(2)}, u32[]{:S(2)}) collective-permute-start(bf16[128,1536]{1,0:T(8,128)(2,1)S(1)} %pad_maximum_fusion.8), channel_id=1, source_target_pairs={{0,8},{8,0},{16,24},{24,16},{1,9},{9,1},{17,25},{25,17},{2,10},{10... | collective-permute-start | bytes 1179656 | tf_op jit(solution)/shard_map/ppermute | solution.py:19
  95.6 12.6 %collective-permute-start.35 = (bf16[128,1536]{1,0:T(8,128)(2,1)S(1)}, bf16[128,1536]{1,0:T(8,128)(2,1)S(1)}, u32[]{:S(2)}, u32[]{:S(2)}) collective-permute-start(bf16[128,1536]{1,0:T(8,128)(2,1)S(1)} %pad_maximum_fusion.9), channel_id=1, source_target_pairs={{0,16},{8,24},{16,0},{24,8},{1,17},{9,25},{17,1},{25,9},{2,18},{10... | collective-permute-start | bytes 1179656 | tf_op jit(solution)/shard_map/ppermute | solution.py:19
  95.9 18.1 %collective-permute-start.15 = (bf16[128,1536]{1,0:T(8,128)(2,1)S(1)}, bf16[128,1536]{1,0:T(8,128)(2,1)S(1)}, u32[]{:S(2)}, u32[]{:S(2)}) collective-permute-start(bf16[128,1536]{1,0:T(8,128)(2,1)S(1)} %pad_maximum_fusion.4), channel_id=1, source_target_pairs={{0,8},{8,0},{16,24},{24,16},{1,9},{9,1},{17,25},{25,17},{2,10},{10... | collective-permute-start | bytes 1179656 | tf_op jit(solution)/shard_map/ppermute | solution.py:19
  99.8 14.3 %collective-permute-start.19 = (bf16[128,1536]{1,0:T(8,128)(2,1)S(1)}, bf16[128,1536]{1,0:T(8,128)(2,1)S(1)}, u32[]{:S(2)}, u32[]{:S(2)}) collective-permute-start(bf16[128,1536]{1,0:T(8,128)(2,1)S(1)} %pad_maximum_fusion.5), channel_id=1, source_target_pairs={{0,16},{8,24},{16,0},{24,8},{1,17},{9,25},{17,1},{25,9},{2,18},{10... | collective-permute-start | bytes 1179656 | tf_op jit(solution)/shard_map/ppermute | solution.py:19
  111.3 5.8 %collective-permute-start.36 = (bf16[256,768]{1,0:T(8,128)(2,1)S(1)}, bf16[256,768]{1,0:T(8,128)(2,1)S(1)}, u32[]{:S(2)}, u32[]{:S(2)}) collective-permute-start(bf16[256,768]{1,0:T(8,128)(2,1)S(1)} %select_convert_fusion), channel_id=1, source_target_pairs={{0,1},{1,0},{2,3},{3,2},{4,5},{5,4},{6,7},{7,6},{8,9},{9,8},{10,11... | collective-permute-start | bytes 1179656 | tf_op jit(solution)/shard_map/ppermute | solution.py:22
  117.0 3.8 %collective-permute-start.20 = (bf16[256,768]{1,0:T(8,128)(2,1)S(1)}, bf16[256,768]{1,0:T(8,128)(2,1)S(1)}, u32[]{:S(2)}, u32[]{:S(2)}) collective-permute-start(bf16[256,768]{1,0:T(8,128)(2,1)S(1)} %select_convert_fusion.1), channel_id=1, source_target_pairs={{0,1},{1,0},{2,3},{3,2},{4,5},{5,4},{6,7},{7,6},{8,9},{9,8},{10,11... | collective-permute-start | bytes 1179656 | tf_op jit(solution)/shard_map/ppermute | solution.py:22
  117.2 5.7 %collective-permute-start.37 = (bf16[64,768]{1,0:T(8,128)(2,1)S(1)}, bf16[64,768]{1,0:T(8,128)(2,1)S(1)}, u32[]{:S(2)}, u32[]{:S(2)}) collective-permute-start(bf16[64,768]{1,0:T(8,128)(2,1)S(1)} %get-tuple-element.42), channel_id=1, source_target_pairs={{0,8},{8,0},{16,24},{24,16},{1,9},{9,1},{17,25},{25,17},{2,10},{10... | collective-permute-start | bytes 294920 | tf_op jit(solution)/shard_map/ppermute | solution.py:19
  117.9 7.2 %collective-permute-start.38 = (bf16[64,768]{1,0:T(8,128)(2,1)S(1)}, bf16[64,768]{1,0:T(8,128)(2,1)S(1)}, u32[]{:S(2)}, u32[]{:S(2)}) collective-permute-start(bf16[64,768]{1,0:T(8,128)(2,1)S(1)} %get-tuple-element.41), channel_id=1, source_target_pairs={{0,16},{8,24},{16,0},{24,8},{1,17},{9,25},{17,1},{25,9},{2,18},{10... | collective-permute-start | bytes 294920 | tf_op jit(solution)/shard_map/ppermute | solution.py:19
  118.4 6.7 %collective-permute-start.39 = (bf16[64,768]{1,0:T(8,128)(2,1)S(1)}, bf16[64,768]{1,0:T(8,128)(2,1)S(1)}, u32[]{:S(2)}, u32[]{:S(2)}) collective-permute-start(bf16[64,768]{1,0:T(8,128)(2,1)S(1)} %get-tuple-element.40), channel_id=1, source_target_pairs={{0,24},{8,16},{16,8},{24,0},{1,25},{9,17},{17,9},{25,1},{2,26},{10... | collective-permute-start | bytes 294920 | tf_op jit(solution)/shard_map/ppermute | solution.py:19
  121.0 8.1 %collective-permute-start.21 = (bf16[64,768]{1,0:T(8,128)(2,1)S(1)}, bf16[64,768]{1,0:T(8,128)(2,1)S(1)}, u32[]{:S(2)}, u32[]{:S(2)}) collective-permute-start(bf16[64,768]{1,0:T(8,128)(2,1)S(1)} %get-tuple-element.30), channel_id=1, source_target_pairs={{0,8},{8,0},{16,24},{24,16},{1,9},{9,1},{17,25},{25,17},{2,10},{10... | collective-permute-start | bytes 294920 | tf_op jit(solution)/shard_map/ppermute | solution.py:19
  121.6 7.5 %collective-permute-start.22 = (bf16[64,768]{1,0:T(8,128)(2,1)S(1)}, bf16[64,768]{1,0:T(8,128)(2,1)S(1)}, u32[]{:S(2)}, u32[]{:S(2)}) collective-permute-start(bf16[64,768]{1,0:T(8,128)(2,1)S(1)} %get-tuple-element.29), channel_id=1, source_target_pairs={{0,16},{8,24},{16,0},{24,8},{1,17},{9,25},{17,1},{25,9},{2,18},{10... | collective-permute-start | bytes 294920 | tf_op jit(solution)/shard_map/ppermute | solution.py:19
  122.9 6.1 %collective-permute-start.23 = (bf16[64,768]{1,0:T(8,128)(2,1)S(1)}, bf16[64,768]{1,0:T(8,128)(2,1)S(1)}, u32[]{:S(2)}, u32[]{:S(2)}) collective-permute-start(bf16[64,768]{1,0:T(8,128)(2,1)S(1)} %get-tuple-element.28), channel_id=1, source_target_pairs={{0,24},{8,16},{16,8},{24,0},{1,25},{9,17},{17,9},{25,1},{2,26},{10... | collective-permute-start | bytes 294920 | tf_op jit(solution)/shard_map/ppermute | solution.py:19
  125.2 15.9 %copy-start = (bf16[128,768]{1,0:T(8,128)(2,1)S(1)}, bf16[128,768]{1,0:T(8,128)(2,1)}, u32[]{:S(2)}) copy-start(bf16[128,768]{1,0:T(8,128)(2,1)} %param.5) | copy-start | bytes 589828
  125.2 7.9 %collective-permute-start.40 = (bf16[32,768]{1,0:T(8,128)(2,1)S(1)}, bf16[32,768]{1,0:T(8,128)(2,1)S(1)}, u32[]{:S(2)}, u32[]{:S(2)}) collective-permute-start(bf16[32,768]{1,0:T(8,128)(2,1)S(1)} %get-tuple-element.35), channel_id=1, source_target_pairs={{0,2},{1,3},{2,4},{3,5},{4,6},{5,7},{6,0},{7,1},{8,10},{9,11},{10,... | collective-permute-start | bytes 147464 | tf_op jit(solution)/shard_map/ppermute | solution.py:25
  125.3 7.8 %collective-permute-start.42 = (bf16[32,768]{1,0:T(8,128)(2,1)S(1)}, bf16[32,768]{1,0:T(8,128)(2,1)S(1)}, u32[]{:S(2)}, u32[]{:S(2)}) collective-permute-start(bf16[32,768]{1,0:T(8,128)(2,1)S(1)} %get-tuple-element.37), channel_id=1, source_target_pairs={{0,6},{1,7},{2,0},{3,1},{4,2},{5,3},{6,4},{7,5},{8,14},{9,15},{10,... | collective-permute-start | bytes 147464 | tf_op jit(solution)/shard_map/ppermute | solution.py:25
  129.2 7.9 %collective-permute-start.24 = (bf16[32,768]{1,0:T(8,128)(2,1)S(1)}, bf16[32,768]{1,0:T(8,128)(2,1)S(1)}, u32[]{:S(2)}, u32[]{:S(2)}) collective-permute-start(bf16[32,768]{1,0:T(8,128)(2,1)S(1)} %get-tuple-element.23), channel_id=1, source_target_pairs={{0,2},{1,3},{2,4},{3,5},{4,6},{5,7},{6,0},{7,1},{8,10},{9,11},{10,... | collective-permute-start | bytes 147464 | tf_op jit(solution)/shard_map/ppermute | solution.py:25
  129.3 7.8 %collective-permute-start.26 = (bf16[32,768]{1,0:T(8,128)(2,1)S(1)}, bf16[32,768]{1,0:T(8,128)(2,1)S(1)}, u32[]{:S(2)}, u32[]{:S(2)}) collective-permute-start(bf16[32,768]{1,0:T(8,128)(2,1)S(1)} %get-tuple-element.25), channel_id=1, source_target_pairs={{0,6},{1,7},{2,0},{3,1},{4,2},{5,3},{6,4},{7,5},{8,14},{9,15},{10,... | collective-permute-start | bytes 147464 | tf_op jit(solution)/shard_map/ppermute | solution.py:25
  133.1 8.0 %collective-permute-start.41 = (bf16[64,768]{1,0:T(8,128)(2,1)S(1)}, bf16[64,768]{1,0:T(8,128)(2,1)S(1)}, u32[]{:S(2)}, u32[]{:S(2)}) collective-permute-start(bf16[64,768]{1,0:T(8,128)(2,1)S(1)} %pad_maximum_fusion.14), channel_id=1, source_target_pairs={{0,2},{1,3},{2,4},{3,5},{4,6},{5,7},{6,0},{7,1},{8,10},{9,11},{10,... | collective-permute-start | bytes 294920 | tf_op jit(solution)/shard_map/ppermute | solution.py:25
  133.2 7.9 %collective-permute-start.43 = (bf16[64,768]{1,0:T(8,128)(2,1)S(1)}, bf16[64,768]{1,0:T(8,128)(2,1)S(1)}, u32[]{:S(2)}, u32[]{:S(2)}) collective-permute-start(bf16[64,768]{1,0:T(8,128)(2,1)S(1)} %pad_maximum_fusion.15), channel_id=1, source_target_pairs={{0,6},{1,7},{2,0},{3,1},{4,2},{5,3},{6,4},{7,5},{8,14},{9,15},{10,... | collective-permute-start | bytes 294920 | tf_op jit(solution)/shard_map/ppermute | solution.py:25
  137.1 6.7 %collective-permute-start.25 = (bf16[64,768]{1,0:T(8,128)(2,1)S(1)}, bf16[64,768]{1,0:T(8,128)(2,1)S(1)}, u32[]{:S(2)}, u32[]{:S(2)}) collective-permute-start(bf16[64,768]{1,0:T(8,128)(2,1)S(1)} %pad_maximum_fusion.12), channel_id=1, source_target_pairs={{0,2},{1,3},{2,4},{3,5},{4,6},{5,7},{6,0},{7,1},{8,10},{9,11},{10,... | collective-permute-start | bytes 294920 | tf_op jit(solution)/shard_map/ppermute | solution.py:25
  137.2 6.7 %collective-permute-start.27 = (bf16[64,768]{1,0:T(8,128)(2,1)S(1)}, bf16[64,768]{1,0:T(8,128)(2,1)S(1)}, u32[]{:S(2)}, u32[]{:S(2)}) collective-permute-start(bf16[64,768]{1,0:T(8,128)(2,1)S(1)} %pad_maximum_fusion.13), channel_id=1, source_target_pairs={{0,6},{1,7},{2,0},{3,1},{4,2},{5,3},{6,4},{7,5},{8,14},{9,15},{10,... | collective-permute-start | bytes 294920 | tf_op jit(solution)/shard_map/ppermute | solution.py:25
where the time goes:
time: 145 us
  starting transfers between devices  75.9 us (52%)
  waiting for transfers between devices  45 us (31%)
  matrix products  11.2 us (8%)
  other arithmetic  7.3 us (5%)
  local copies, waits for them, and re-layouts  4.59 us (3%)
    ppermute x25, starting transfers between devices, over_rows(): return lax.ppermute(value, 'rows', [(i, i ^ flip) for i in range(rows)])  45.3 us
    ppermute x25, waiting for transfers between devices, over_rows(): return lax.ppermute(value, 'rows', [(i, i ^ flip) for i in range(rows)])  32.8 us
    ppermute x11, starting transfers between devices, over_depth(): lax.ppermute(value, 'mp', [(i, (i + CORES * shift) % mp) for i in range(m...  20.2 us
    ppermute x4, starting transfers between devices, spread(): return lax.ppermute(value, ('rows', 'mp'), pairs)  9.65 us
    ppermute x4, waiting for transfers between devices, spread(): return lax.ppermute(value, ('rows', 'mp'), pairs)  6.53 us
    dot_general x4, matrix products, body(): jnp.dot(block, weight_out[cols], preferred_element_type=jnp.float32)  5.71 us
    dot_general x4, matrix products, body(): jnp.dot(x_here, weight_in[:, cols], preferred_element_type=jnp.float32)  5.52 us
    convert_element_type x2, other arithmetic, body(): jax.nn.gelu(held[0] + hidden_bias[None, cols], approximate=False)  3.61 us
  transfers between devices with their start and end apart: 44, of which 20 were waited for; matrix products, arithmetic and copies ran while one was open for 10% of the time, Pallas kernels for 0%

commit v1 on v0

--- a/solution.py
+++ b/solution.py
@@ -7,7 +7,12 @@
 floor_value = 0.1
 CORES = 2
 TOKEN_CHUNKS = 2
-COLUMN_CHUNKS = 2
+COLUMN_CHUNKS = 3
+HALVES = True
+
+
+def joined(parts, axis):
+    return parts[0] if len(parts) == 1 else jnp.concatenate(parts, axis=axis)
 
 
 def make_body(rows, mp):
@@ -57,12 +62,13 @@
         features = width * mp
         row, place = lax.axis_index("rows"), lax.axis_index("mp")
         core, chip = place % CORES, place // CORES
+        first = core == 0
 
         as_float = tokens.astype(jnp.float32)
         sums = jnp.stack([jnp.sum(as_float, axis=1), jnp.sum(as_float * as_float, axis=1)])
-        sums = sums + over_cores(sums)
-        sums = jnp.stack([over_rows(sums, flip) if flip else sums for flip in range(rows)])
-        sums = sum([over_depth(sums, shift) for shift in range(1, depth)], sums)
+        sums = lax.all_to_all(jnp.broadcast_to(sums, (rows * mp,) + sums.shape), ("rows", "mp"), 0, 0)
+        sums = jnp.sum(sums.reshape((rows, mp) + sums.shape[1:]), axis=1)
+        sums = jnp.stack([lax.dynamic_index_in_dim(sums, row ^ flip, 0, keepdims=False) for flip in range(rows)])
         row_mean = sums[:, 0] / features
         row_var = jnp.maximum(sums[:, 1] / features - row_mean * row_mean, 0.0)
         inverse = lax.rsqrt(row_var + floor_value)
@@ -83,51 +89,62 @@
                 scaled = (raw - row_mean[flip][:, None]) * inverse[flip][:, None] * gains[sub][None, :]
                 parts.append(scaled.astype(jnp.bfloat16))
             pieces.append(parts)
-        x_own = [jnp.concatenate([p[sub] for p in pieces], axis=0) for sub in range(per_row)]
-        x_own = x_own[0] if per_row == 1 else jnp.concatenate(x_own, axis=1)
+        x_own = joined([jnp.concatenate([p[sub] for p in pieces], axis=0) for sub in range(per_row)], 1)
         x_other = over_cores(x_own)
-        first = core == 0
-        columns = []
-        for sub in range(per_row):
-            at = slice(sub * width, (sub + 1) * width)
-            columns.append(jnp.where(first, x_own[:, at], x_other[:, at]))
-            columns.append(jnp.where(first, x_other[:, at], x_own[:, at]))
-        x_all = jnp.concatenate(columns, axis=1).reshape(rows, count, features // rows)
+
+        if HALVES:
+            blocks_in = weight_in.reshape(per_row, CORES, width, hidden_width)
+            w_own = lax.dynamic_index_in_dim(blocks_in, core, 1, keepdims=False).reshape(per_row * width, hidden_width)
+            w_other = lax.dynamic_index_in_dim(blocks_in, 1 - core, 1, keepdims=False).reshape(per_row * width, hidden_width)
+            w_own, w_other = lax.optimization_barrier((w_own, w_other))
+            x_all = [x.reshape(rows, count, per_row * width) for x in (x_own, x_other)]
+            w_all = [w_own, w_other]
+        else:
+            columns = []
+            for sub in range(per_row):
+                at = slice(sub * width, (sub + 1) * width)
+                columns.append(jnp.where(first, x_own[:, at], x_other[:, at]))
+                columns.append(jnp.where(first, x_other[:, at], x_own[:, at]))
+            x_all = [jnp.concatenate(columns, axis=1).reshape(rows, count, features // rows)]
+            w_all = [weight_in]
 
         rows_here = count // TOKEN_CHUNKS
         cols_here = hidden_width // COLUMN_CHUNKS
         results = []
         for t in range(TOKEN_CHUNKS):
             span = slice(t * rows_here, (t + 1) * rows_here)
-            x_here = x_all[:, span].reshape(rows * rows_here, features // rows)
             terms = 0.0
             for c in range(COLUMN_CHUNKS):
                 cols = slice(c * cols_here, (c + 1) * cols_here)
-                order = bits[c % len(bits):] + bits[: c % len(bits)]
-                part = jnp.dot(x_here, weight_in[:, cols], preferred_element_type=jnp.float32)
+                turn = (c + t) % len(bits)
+                order = bits[turn:] + bits[:turn]
+                part = 0.0
+                for x, w in zip(x_all, w_all):
+                    x = x[:, span].reshape(rows * rows_here, x.shape[2])
+                    part = part + jnp.dot(x, w[:, cols], preferred_element_type=jnp.float32)
                 held = {b: part[b * rows_here : (b + 1) * rows_here] for b in range(rows)}
                 for bit in order:
                     going = [b for b in held if b & bit]
                     sent = over_rows(jnp.concatenate([held[b].astype(jnp.bfloat16) for b in going], axis=0), bit)
                     held = {
-                        b ^ bit: held[b ^ bit] + sent[n * rows_here : (n + 1) * rows_here].astype(jnp.float32)
-                        for n, b in enumerate(going)
+                        b ^ bit: held[b ^ bit] + sent[k * rows_here : (k + 1) * rows_here].astype(jnp.float32)
+                        for k, b in enumerate(going)
                     }
                 hidden = jax.nn.gelu(held[0] + hidden_bias[None, cols], approximate=False).astype(jnp.bfloat16)
                 names, block = [0], hidden
                 for bit in reversed(order):
                     names = names + [b ^ bit for b in names]
-                    block = jnp.concatenate([block, over_rows(block, bit)], axis=0)
+                    more = over_rows(block, bit)
+                    block = jnp.concatenate([block, more], axis=0)
                 places = {b: n for n, b in enumerate(names)}
                 if names != sorted(names):
                     block = jnp.concatenate([block[places[b] * rows_here : (places[b] + 1) * rows_here] for b in range(rows)], axis=0)
                 terms = terms + jnp.dot(block, weight_out[cols], preferred_element_type=jnp.float32)
 
             terms = [terms[:, n * width : (n + 1) * width] for n in range(per_row * CORES)]
-            lower = terms[0::CORES][0] if per_row == 1 else jnp.concatenate(terms[0::CORES], axis=1)
-            upper = terms[1::CORES][0] if per_row == 1 else jnp.concatenate(terms[1::CORES], axis=1)
-            given = jnp.where(first, upper, lower).astype(jnp.bfloat16)
-            total = jnp.where(first, lower, upper) + over_cores(given).astype(jnp.float32)
+            lower, upper = joined(terms[0::CORES], 1), joined(terms[1::CORES], 1)
+            taken = over_cores(jnp.where(first, upper, lower).astype(jnp.bfloat16))
+            total = jnp.where(first, lower, upper) + taken.astype(jnp.float32)
             backs = []
             for flip in range(rows):
                 piece = total[flip * rows_here : (flip + 1) * rows_here].astype(jnp.bfloat16)
@@ -140,7 +157,7 @@
                 index = ((target // per_row) ^ row) * per_row + target % per_row
                 parts.append(lax.dynamic_index_in_dim(blocks, index, 0, keepdims=False).astype(jnp.float32))
             results.append((as_float[span] + scatter_depth(parts)).astype(jnp.bfloat16))
-        return results[0] if TOKEN_CHUNKS == 1 else jnp.concatenate(results, axis=0)
+        return joined(results, 0)
 
     return body
 

time: 145 us -> 127 us (0.88)
  waiting for transfers between devices: 45 us -> 27.3 us
  starting transfers between devices: 75.9 us -> 65.7 us
  local copies, waits for them, and re-layouts: 4.59 us -> 12.4 us
  matrix products: 11.2 us -> 13.1 us
    ppermute x25 -> x30, waiting for transfers between devices: 32.8 us -> 20.8 us  [over_rows(): return lax.ppermute(value, 'rows', [(i, i ^ flip) for i in range(rows)])]
    ppermute x25 -> x30, starting transfers between devices: 45.3 us -> 33.9 us  [over_rows(): return lax.ppermute(value, 'rows', [(i, i ^ flip) for i in range(rows)])]
    reshape x0 -> x1, local copies, waits for them, and re-layouts: none -> 8.3 us  [body(): lax.dynamic_index_in_dim(blocks_in, 1 - core, 1, keepdims=False)]
    ppermute x4, waiting for transfers between devices: 6.53 us -> 0.01 us  [spread(): return lax.ppermute(value, ('rows', 'mp'), pairs)]
    ppermute x11 -> x8, starting transfers between devices: 20.2 us -> 15.6 us  [over_depth(): lax.ppermute(value, 'mp', [(i, (i + CORES * shift) % mp) for i in range(m...]
    all_to_all x0 -> x1, starting transfers between devices: none -> 4.19 us  [body(): lax.all_to_all(jnp.broadcast_to(sums, (rows * mp,) + sums.shape), ('rows'...]
    all_to_all x0 -> x1, waiting for transfers between devices: none -> 3.69 us  [body(): lax.all_to_all(jnp.broadcast_to(sums, (rows * mp,) + sums.shape), ('rows'...]
    ppermute x4 -> x3, waiting for transfers between devices: 2.85 us -> 0.01 us  [over_cores(): return lax.ppermute(value, 'mp', [(i, i ^ 1) for i in range(mp)])]
  transfers between devices with their start and end apart: 44 -> 46, of which waited for: 20 -> 14; matrix products, arithmetic and copies ran while one was open for 10% -> 23% of each run, Pallas kernels for 0% -> 0%
where the time goes in v1:
time: 127 us; the launch traced here: 126 us
  starting transfers between devices  65.7 us (52%)
  waiting for transfers between devices  27.3 us (21%)
  matrix products  13.1 us (10%)
  local copies, waits for them, and re-layouts  12.4 us (10%)
  other arithmetic  7.19 us (6%)
    ppermute x30, starting transfers between devices, over_rows(): return lax.ppermute(value, 'rows', [(i, i ^ flip) for i in range(rows)])  33.9 us
    ppermute x30, waiting for transfers between devices, over_rows(): return lax.ppermute(value, 'rows', [(i, i ^ flip) for i in range(rows)])  20.8 us
    ppermute x8, starting transfers between devices, over_depth(): lax.ppermute(value, 'mp', [(i, (i + CORES * shift) % mp) for i in range(m...  15.6 us
    ppermute x4, starting transfers between devices, spread(): return lax.ppermute(value, ('rows', 'mp'), pairs)  11.8 us
    reshape x1, local copies, waits for them, and re-layouts, body(): lax.dynamic_index_in_dim(blocks_in, 1 - core, 1, keepdims=False)  8.3 us
    dot_general x12, matrix products, body(): part = part + jnp.dot(x, w[:, cols], preferred_element_type=jnp.float32)  7.08 us
    dot_general x6, matrix products, body(): jnp.dot(block, weight_out[cols], preferred_element_type=jnp.float32)  5.98 us
    all_to_all x1, starting transfers between devices, body(): lax.all_to_all(jnp.broadcast_to(sums, (rows * mp,) + sums.shape), ('rows'...  4.19 us
  transfers between devices with their start and end apart: 46, of which 14 were waited for; matrix products, arithmetic and copies ran while one was open for 23% of the time, Pallas kernels for 0%

profile of v1, /device:TPU:0, one launch (start us, length us, event | category | flops | bytes accessed | tf_op | source)
XLA Modules:
  0.0 126.5 jit_solution(1720443465322983824)
XLA Ops:
  0.0 1.6 %collective-permute-start = (bf16[128,768]{1,0:T(8,128)(2,1)}, bf16[128,768]{1,0:T(8,128)(2,1)S(1)}, u32[]{:S(2)}, u32[]{:S(2)}) collective-permute-start(bf16[128,768]{1,0:T(8,128)(2,1)} %param.5), channel_id=1, source_target_pairs={{0,0},{1,1},{2,8},{3,9},{4,16},{5,17},{6,24},{7,25},{8,2},{9,3},{1... | collective-permute-start | bytes 589832 | tf_op jit(solution)/shard_map/ppermute | solution.py:39
  1.6 4.8 %collective-permute-start.1 = (bf16[128,768]{1,0:T(8,128)(2,1)}, bf16[128,768]{1,0:T(8,128)(2,1)S(1)}, u32[]{:S(2)}, u32[]{:S(2)}) collective-permute-start(bf16[128,768]{1,0:T(8,128)(2,1)} %param.5), channel_id=1, source_target_pairs={{0,2},{1,3},{2,10},{3,11},{4,18},{5,19},{6,26},{7,27},{8,0},{9,1},... | collective-permute-start | bytes 589832 | tf_op jit(solution)/shard_map/ppermute | solution.py:39
  6.4 3.5 %collective-permute-start.2 = (bf16[128,768]{1,0:T(8,128)(2,1)}, bf16[128,768]{1,0:T(8,128)(2,1)S(1)}, u32[]{:S(2)}, u32[]{:S(2)}) collective-permute-start(bf16[128,768]{1,0:T(8,128)(2,1)} %param.5), channel_id=1, source_target_pairs={{0,4},{1,5},{2,12},{3,13},{4,20},{5,21},{6,28},{7,29},{8,6},{9,7},... | collective-permute-start | bytes 589832 | tf_op jit(solution)/shard_map/ppermute | solution.py:39
  9.9 1.9 %collective-permute-start.3 = (bf16[128,768]{1,0:T(8,128)(2,1)}, bf16[128,768]{1,0:T(8,128)(2,1)S(1)}, u32[]{:S(2)}, u32[]{:S(2)}) collective-permute-start(bf16[128,768]{1,0:T(8,128)(2,1)} %param.5), channel_id=1, source_target_pairs={{0,6},{1,7},{2,14},{3,15},{4,22},{5,23},{6,30},{7,31},{8,4},{9,5},... | collective-permute-start | bytes 589832 | tf_op jit(solution)/shard_map/ppermute | solution.py:39
  11.8 1.1 convert_reduce_fusion
  12.9 0.6 broadcast_in_dim.2
  13.5 4.2 %all-to-all-start = ((f32[32,2,128]{2,1,0:T(2,128)}), f32[32,2,128]{2,1,0:T(2,128)S(1)}, u32[]{:S(2)}, u32[]{:S(2)}) async-start(f32[32,2,128]{2,1,0:T(2,128)} %broadcast_in_dim.2), calls=%async_computation | async-start | bytes 65536 | tf_op jit(solution)/shard_map/all_to_all | solution.py:69
  17.8 8.3 %dynamic-slice_bitcast_fusion = (bf16[768,3072]{1,0:T(8,128)(2,1)}, bf16[768,3072]{1,0:T(8,128)(2,1)}) fusion(bf16[1,2,768,3072]{3,2,1,0:T(8,128)(2,1)} %bitcast.113, s32[]{:T(128)S(6)} %select_n.147, s32[]{:T(128)S(6)} %select_n.143), kind=kLoop, calls=%fused_computation | loop fusion | bytes 18874376 | tf_op jit(solution)/shard_map/reshape | solution.py:98
  26.1 0.8 dynamic_slice.70
  26.9 3.7 %all-to-all-done = f32[32,2,128]{2,1,0:T(2,128)S(1)} async-done(((f32[32,2,128]{2,1,0:T(2,128)}), f32[32,2,128]{2,1,0:T(2,128)S(1)}, u32[]{:S(2)}, u32[]{:S(2)}) %all-to-all-start) | async-done | bytes 32800 | tf_op jit(solution)/shard_map/all_to_all | solution.py:69
  31.4 1.6 %copy-done = bf16[768,3072]{1,0:T(8,128)(2,1)S(1)} copy-done((bf16[768,3072]{1,0:T(8,128)(2,1)S(1)}, bf16[768,3072]{1,0:T(8,128)(2,1)}, u32[]{:S(2)}) %copy-start) | copy-done | bytes 4718616
  37.9 0.7 collective-permute-start.25
  39.2 1.4 %collective-permute-start.5 = (bf16[128,1024]{1,0:T(8,128)(2,1)S(1)}, bf16[128,1024]{1,0:T(8,128)(2,1)S(1)}, u32[]{:S(2)}, u32[]{:S(2)}) collective-permute-start(bf16[128,1024]{1,0:T(8,128)(2,1)S(1)} %pad_maximum_fusion.4), channel_id=1, source_target_pairs={{0,8},{8,0},{16,24},{24,16},{1,9},{9,1},{17,25},{25,17},{2,10},{10... | collective-permute-start | bytes 786440 | tf_op jit(solution)/shard_map/ppermute | solution.py:24
  41.3 0.7 collective-permute-start.29
  42.7 1.5 %collective-permute-start.9 = (bf16[128,1024]{1,0:T(8,128)(2,1)S(1)}, bf16[128,1024]{1,0:T(8,128)(2,1)S(1)}, u32[]{:S(2)}, u32[]{:S(2)}) collective-permute-start(bf16[128,1024]{1,0:T(8,128)(2,1)S(1)} %slice.719), channel_id=1, source_target_pairs={{0,16},{8,24},{16,0},{24,8},{1,17},{9,25},{17,1},{25,9},{2,18},{10... | collective-permute-start | bytes 786440 | tf_op jit(solution)/shard_map/ppermute | solution.py:24
  44.2 0.6 fusion.55
  44.8 0.7 collective-permute-start.33
  46.2 1.0 collective-permute-done.25
  47.1 1.4 %collective-permute-start.13 = (bf16[128,1024]{1,0:T(8,128)(2,1)S(1)}, bf16[128,1024]{1,0:T(8,128)(2,1)S(1)}, u32[]{:S(2)}, u32[]{:S(2)}) collective-permute-start(bf16[128,1024]{1,0:T(8,128)(2,1)S(1)} %pad_maximum_fusion.7), channel_id=1, source_target_pairs={{0,8},{8,0},{16,24},{24,16},{1,9},{9,1},{17,25},{25,17},{2,10},{10... | collective-permute-start | bytes 786440 | tf_op jit(solution)/shard_map/ppermute | solution.py:24
  48.6 1.2 collective-permute-start.26
  49.9 4.2 %collective-permute-done.29 = bf16[128,1024]{1,0:T(8,128)(2,1)S(1)} collective-permute-done((bf16[128,1024]{1,0:T(8,128)(2,1)S(1)}, bf16[128,1024]{1,0:T(8,128)(2,1)S(1)}, u32[]{:S(2)}, u32[]{:S(2)}) %collective-permute-start.29) | collective-permute-done | bytes 262176 | tf_op jit(solution)/shard_map/ppermute | solution.py:24
  54.1 1.4 %collective-permute-start.6 = (bf16[64,1024]{1,0:T(8,128)(2,1)S(1)}, bf16[64,1024]{1,0:T(8,128)(2,1)S(1)}, u32[]{:S(2)}, u32[]{:S(2)}) collective-permute-start(bf16[64,1024]{1,0:T(8,128)(2,1)S(1)} %fusion.139), channel_id=1, source_target_pairs={{0,16},{8,24},{16,0},{24,8},{1,17},{9,25},{17,1},{25,9},{2,18},{10... | collective-permute-start | bytes 393224 | tf_op jit(solution)/shard_map/ppermute | solution.py:24
  55.6 0.7 collective-permute-start.30
  56.3 2.1 %collective-permute-done.33 = bf16[128,1024]{1,0:T(8,128)(2,1)S(1)} collective-permute-done((bf16[128,1024]{1,0:T(8,128)(2,1)S(1)}, bf16[128,1024]{1,0:T(8,128)(2,1)S(1)}, u32[]{:S(2)}, u32[]{:S(2)}) %collective-permute-start.33) | collective-permute-done | bytes 262176 | tf_op jit(solution)/shard_map/ppermute | solution.py:24
  58.4 1.4 %collective-permute-start.10 = (bf16[64,1024]{1,0:T(8,128)(2,1)S(1)}, bf16[64,1024]{1,0:T(8,128)(2,1)S(1)}, u32[]{:S(2)}, u32[]{:S(2)}) collective-permute-start(bf16[64,1024]{1,0:T(8,128)(2,1)S(1)} %fusion.136), channel_id=1, source_target_pairs={{0,8},{8,0},{16,24},{24,16},{1,9},{9,1},{17,25},{25,17},{2,10},{10... | collective-permute-start | bytes 393224 | tf_op jit(solution)/shard_map/ppermute | solution.py:24
  59.9 1.2 collective-permute-start.34
  61.1 1.4 %collective-permute-done.26 = bf16[64,1024]{1,0:T(8,128)(2,1)S(1)} collective-permute-done((bf16[64,1024]{1,0:T(8,128)(2,1)S(1)}, bf16[64,1024]{1,0:T(8,128)(2,1)S(1)}, u32[]{:S(2)}, u32[]{:S(2)}) %collective-permute-start.26) | collective-permute-done | bytes 131104 | tf_op jit(solution)/shard_map/ppermute | solution.py:24
  62.5 1.4 %collective-permute-start.14 = (bf16[64,1024]{1,0:T(8,128)(2,1)S(1)}, bf16[64,1024]{1,0:T(8,128)(2,1)S(1)}, u32[]{:S(2)}, u32[]{:S(2)}) collective-permute-start(bf16[64,1024]{1,0:T(8,128)(2,1)S(1)} %fusion.133), channel_id=1, source_target_pairs={{0,16},{8,24},{16,0},{24,8},{1,17},{9,25},{17,1},{25,9},{2,18},{10... | collective-permute-start | bytes 393224 | tf_op jit(solution)/shard_map/ppermute | solution.py:24
  63.9 1.2 fusion.108
  65.2 1.5 %collective-permute-start.27 = (bf16[64,1024]{1,0:T(8,128)(2,1)S(1)}, bf16[64,1024]{1,0:T(8,128)(2,1)S(1)}, u32[]{:S(2)}, u32[]{:S(2)}) collective-permute-start(bf16[64,1024]{1,0:T(8,128)(2,1)S(1)} %get-tuple-element.59), channel_id=1, source_target_pairs={{0,8},{8,0},{16,24},{24,16},{1,9},{9,1},{17,25},{25,17},{2,10},{10... | collective-permute-start | bytes 393224 | tf_op jit(solution)/shard_map/ppermute | solution.py:24
  66.7 1.2 fusion.111
  68.5 1.4 %fusion.114 = (bf16[64,1024]{1,0:T(8,128)(2,1)S(1)}, bf16[64,1024]{1,0:T(8,128)(2,1)S(1)}) fusion(bf16[64,1024]{1,0:T(8,128)(2,1)S(1)} %collective-permute-done.14, f32[256,1024]{1,0:T(8,128)S(1)} %get-tuple-element.81, bf16[128,1024]{1,0:T(8,128)(2,1)S(1)} %collective-permute-done.13, f32[1024]{0:T(1024)S(1)} %get-tuple-element.56, ...), kind=kLoop, calls=%fused_computation.124 | loop fusion | flops 9175040 | bytes 1314816 | tf_op jit(solution)/shard_map/convert_element_type | solution.py:133
  69.9 1.1 collective-permute-start.35
  71.0 1.5 %collective-permute-start.7 = (bf16[64,1024]{1,0:T(8,128)(2,1)S(1)}, bf16[64,1024]{1,0:T(8,128)(2,1)S(1)}, u32[]{:S(2)}, u32[]{:S(2)}) collective-permute-start(bf16[64,1024]{1,0:T(8,128)(2,1)S(1)} %get-tuple-element.58), channel_id=1, source_target_pairs={{0,16},{8,24},{16,0},{24,8},{1,17},{9,25},{17,1},{25,9},{2,18},{10... | collective-permute-start | bytes 393224 | tf_op jit(solution)/shard_map/ppermute | solution.py:24
  72.5 1.0 collective-permute-start.11
  74.3 1.3 %collective-permute-start.28 = (bf16[128,1024]{1,0:T(8,128)(2,1)S(1)}, bf16[128,1024]{1,0:T(8,128)(2,1)S(1)}, u32[]{:S(2)}, u32[]{:S(2)}) collective-permute-start(bf16[128,1024]{1,0:T(8,128)(2,1)S(1)} %pad_maximum_fusion.9), channel_id=1, source_target_pairs={{0,16},{8,24},{16,0},{24,8},{1,17},{9,25},{17,1},{25,9},{2,18},{10... | collective-permute-start | bytes 786440 | tf_op jit(solution)/shard_map/ppermute | solution.py:24
  76.0 0.7 collective-permute-start.32
  76.7 0.6 collective-permute-done.7
  77.3 1.5 %collective-permute-start.36 = (bf16[128,1024]{1,0:T(8,128)(2,1)S(1)}, bf16[128,1024]{1,0:T(8,128)(2,1)S(1)}, u32[]{:S(2)}, u32[]{:S(2)}) collective-permute-start(bf16[128,1024]{1,0:T(8,128)(2,1)S(1)} %pad_maximum_fusion.12), channel_id=1, source_target_pairs={{0,16},{8,24},{16,0},{24,8},{1,17},{9,25},{17,1},{25,9},{2,18},{10... | collective-permute-start | bytes 786440 | tf_op jit(solution)/shard_map/ppermute | solution.py:24
  78.9 1.1 collective-permute-start.8
  80.1 1.5 %collective-permute-start.12 = (bf16[128,1024]{1,0:T(8,128)(2,1)S(1)}, bf16[128,1024]{1,0:T(8,128)(2,1)S(1)}, u32[]{:S(2)}, u32[]{:S(2)}) collective-permute-start(bf16[128,1024]{1,0:T(8,128)(2,1)S(1)} %pad_maximum_fusion.6), channel_id=1, source_target_pairs={{0,16},{8,24},{16,0},{24,8},{1,17},{9,25},{17,1},{25,9},{2,18},{10... | collective-permute-start | bytes 786440 | tf_op jit(solution)/shard_map/ppermute | solution.py:24
  81.7 3.5 %collective-permute-done.32 = bf16[128,1024]{1,0:T(8,128)(2,1)S(1)} collective-permute-done((bf16[128,1024]{1,0:T(8,128)(2,1)S(1)}, bf16[128,1024]{1,0:T(8,128)(2,1)S(1)}, u32[]{:S(2)}, u32[]{:S(2)}) %collective-permute-start.32) | collective-permute-done | bytes 262176 | tf_op jit(solution)/shard_map/ppermute | solution.py:24
  85.2 0.7 collective-permute-start.16
  85.9 1.0 fusion.4
  86.9 4.4 %collective-permute-done.36 = bf16[128,1024]{1,0:T(8,128)(2,1)S(1)} collective-permute-done((bf16[128,1024]{1,0:T(8,128)(2,1)S(1)}, bf16[128,1024]{1,0:T(8,128)(2,1)S(1)}, u32[]{:S(2)}, u32[]{:S(2)}) %collective-permute-start.36) | collective-permute-done | bytes 262176 | tf_op jit(solution)/shard_map/ppermute | solution.py:24
  91.4 1.0 fusion
  92.4 1.1 fusion.13
  93.6 1.4 %collective-permute-done.12 = bf16[128,1024]{1,0:T(8,128)(2,1)S(1)} collective-permute-done((bf16[128,1024]{1,0:T(8,128)(2,1)S(1)}, bf16[128,1024]{1,0:T(8,128)(2,1)S(1)}, u32[]{:S(2)}, u32[]{:S(2)}) %collective-permute-start.12) | collective-permute-done | bytes 262176 | tf_op jit(solution)/shard_map/ppermute | solution.py:24
  95.0 1.0 fusion.6
  96.0 1.0 fusion.2
  97.0 1.0 fusion.10
  98.3 0.8 collective-permute-start.38
  99.1 1.2 collective-permute-start.39
  100.4 1.5 %collective-permute-start.40 = (bf16[64,768]{1,0:T(8,128)(2,1)S(1)}, bf16[64,768]{1,0:T(8,128)(2,1)S(1)}, u32[]{:S(2)}, u32[]{:S(2)}) collective-permute-start(bf16[64,768]{1,0:T(8,128)(2,1)S(1)} %get-tuple-element.46), channel_id=1, source_target_pairs={{0,24},{8,16},{16,8},{24,0},{1,25},{9,17},{17,9},{25,1},{2,26},{10... | collective-permute-start | bytes 294920 | tf_op jit(solution)/shard_map/ppermute | solution.py:24
  102.1 0.8 collective-permute-start.18
  102.9 1.2 collective-permute-start.19
  104.1 1.5 %collective-permute-start.20 = (bf16[64,768]{1,0:T(8,128)(2,1)S(1)}, bf16[64,768]{1,0:T(8,128)(2,1)S(1)}, u32[]{:S(2)}, u32[]{:S(2)}) collective-permute-start(bf16[64,768]{1,0:T(8,128)(2,1)S(1)} %get-tuple-element.36), channel_id=1, source_target_pairs={{0,24},{8,16},{16,8},{24,0},{1,25},{9,17},{17,9},{25,1},{2,26},{10... | collective-permute-start | bytes 294920 | tf_op jit(solution)/shard_map/ppermute | solution.py:24
  105.7 1.3 %collective-permute-done.40 = bf16[64,768]{1,0:T(8,128)(2,1)S(1)} collective-permute-done((bf16[64,768]{1,0:T(8,128)(2,1)S(1)}, bf16[64,768]{1,0:T(8,128)(2,1)S(1)}, u32[]{:S(2)}, u32[]{:S(2)}) %collective-permute-start.40) | collective-permute-done | bytes 98336 | tf_op jit(solution)/shard_map/ppermute | solution.py:24
  107.6 3.3 %collective-permute-start.43 = (bf16[32,768]{1,0:T(8,128)(2,1)S(1)}, bf16[32,768]{1,0:T(8,128)(2,1)S(1)}, u32[]{:S(2)}, u32[]{:S(2)}) collective-permute-start(bf16[32,768]{1,0:T(8,128)(2,1)S(1)} %get-tuple-element.43), channel_id=1, source_target_pairs={{0,6},{1,7},{2,0},{3,1},{4,2},{5,3},{6,4},{7,5},{8,14},{9,15},{10,... | collective-permute-start | bytes 147464 | tf_op jit(solution)/shard_map/ppermute | solution.py:30
  111.1 3.8 %collective-permute-start.23 = (bf16[32,768]{1,0:T(8,128)(2,1)S(1)}, bf16[32,768]{1,0:T(8,128)(2,1)S(1)}, u32[]{:S(2)}, u32[]{:S(2)}) collective-permute-start(bf16[32,768]{1,0:T(8,128)(2,1)S(1)} %get-tuple-element.33), channel_id=1, source_target_pairs={{0,6},{1,7},{2,0},{3,1},{4,2},{5,3},{6,4},{7,5},{8,14},{9,15},{10,... | collective-permute-start | bytes 147464 | tf_op jit(solution)/shard_map/ppermute | solution.py:30
  115.0 3.8 %collective-permute-start.44 = (bf16[64,768]{1,0:T(8,128)(2,1)S(1)}, bf16[64,768]{1,0:T(8,128)(2,1)S(1)}, u32[]{:S(2)}, u32[]{:S(2)}) collective-permute-start(bf16[64,768]{1,0:T(8,128)(2,1)S(1)} %pad_maximum_fusion.17), channel_id=1, source_target_pairs={{0,6},{1,7},{2,0},{3,1},{4,2},{5,3},{6,4},{7,5},{8,14},{9,15},{10,... | collective-permute-start | bytes 294920 | tf_op jit(solution)/shard_map/ppermute | solution.py:30
  119.0 3.8 %collective-permute-start.24 = (bf16[64,768]{1,0:T(8,128)(2,1)S(1)}, bf16[64,768]{1,0:T(8,128)(2,1)S(1)}, u32[]{:S(2)}, u32[]{:S(2)}) collective-permute-start(bf16[64,768]{1,0:T(8,128)(2,1)S(1)} %pad_maximum_fusion.15), channel_id=1, source_target_pairs={{0,6},{1,7},{2,0},{3,1},{4,2},{5,3},{6,4},{7,5},{8,14},{9,15},{10,... | collective-permute-start | bytes 294920 | tf_op jit(solution)/shard_map/ppermute | solution.py:30
  122.9 2.8 %collective-permute-done.22 = bf16[64,768]{1,0:T(8,128)(2,1)S(1)} collective-permute-done((bf16[64,768]{1,0:T(8,128)(2,1)S(1)}, bf16[64,768]{1,0:T(8,128)(2,1)S(1)}, u32[]{:S(2)}, u32[]{:S(2)}) %collective-permute-start.22) | collective-permute-done | bytes 98336 | tf_op jit(solution)/shard_map/ppermute | solution.py:30
  125.8 0.7 pad_maximum_fusion.13
  (128 shorter events, 12.3 us)
Async XLA Ops:
  0.0 30.7 %collective-permute-start = (bf16[128,768]{1,0:T(8,128)(2,1)}, bf16[128,768]{1,0:T(8,128)(2,1)S(1)}, u32[]{:S(2)}, u32[]{:S(2)}) collective-permute-start(bf16[128,768]{1,0:T(8,128)(2,1)} %param.5), channel_id=1, source_target_pairs={{0,0},{1,1},{2,8},{3,9},{4,16},{5,17},{6,24},{7,25},{8,2},{9,3},{1... | collective-permute-start | bytes 589832 | tf_op jit(solution)/shard_map/ppermute | solution.py:39
  1.6 29.1 %collective-permute-start.1 = (bf16[128,768]{1,0:T(8,128)(2,1)}, bf16[128,768]{1,0:T(8,128)(2,1)S(1)}, u32[]{:S(2)}, u32[]{:S(2)}) collective-permute-start(bf16[128,768]{1,0:T(8,128)(2,1)} %param.5), channel_id=1, source_target_pairs={{0,2},{1,3},{2,10},{3,11},{4,18},{5,19},{6,26},{7,27},{8,0},{9,1},... | collective-permute-start | bytes 589832 | tf_op jit(solution)/shard_map/ppermute | solution.py:39
  6.4 24.3 %collective-permute-start.2 = (bf16[128,768]{1,0:T(8,128)(2,1)}, bf16[128,768]{1,0:T(8,128)(2,1)S(1)}, u32[]{:S(2)}, u32[]{:S(2)}) collective-permute-start(bf16[128,768]{1,0:T(8,128)(2,1)} %param.5), channel_id=1, source_target_pairs={{0,4},{1,5},{2,12},{3,13},{4,20},{5,21},{6,28},{7,29},{8,6},{9,7},... | collective-permute-start | bytes 589832 | tf_op jit(solution)/shard_map/ppermute | solution.py:39
  9.9 20.8 %collective-permute-start.3 = (bf16[128,768]{1,0:T(8,128)(2,1)}, bf16[128,768]{1,0:T(8,128)(2,1)S(1)}, u32[]{:S(2)}, u32[]{:S(2)}) collective-permute-start(bf16[128,768]{1,0:T(8,128)(2,1)} %param.5), channel_id=1, source_target_pairs={{0,6},{1,7},{2,14},{3,15},{4,22},{5,23},{6,30},{7,31},{8,4},{9,5},... | collective-permute-start | bytes 589832 | tf_op jit(solution)/shard_map/ppermute | solution.py:39
  13.5 17.0 %all-to-all-start = ((f32[32,2,128]{2,1,0:T(2,128)}), f32[32,2,128]{2,1,0:T(2,128)S(1)}, u32[]{:S(2)}, u32[]{:S(2)}) async-start(f32[32,2,128]{2,1,0:T(2,128)} %broadcast_in_dim.2), calls=%async_computation | async-start | bytes 65536 | tf_op jit(solution)/shard_map/all_to_all | solution.py:69
  17.7 8.3 %copy-start.2 = (f32[3072]{0:T(1024)S(1)}, f32[3072]{0:T(1024)}, u32[]{:S(2)}) copy-start(f32[3072]{0:T(1024)} %param.7) | copy-start | bytes 36868
  30.7 2.3 %copy-start = (bf16[768,3072]{1,0:T(8,128)(2,1)S(1)}, bf16[768,3072]{1,0:T(8,128)(2,1)}, u32[]{:S(2)}) copy-start(bf16[768,3072]{1,0:T(8,128)(2,1)} %get-tuple-element.7) | copy-start | bytes 14155780
  31.2 5.4 %collective-permute-start.4 = (bf16[512,768]{1,0:T(8,128)(2,1)S(1)}, bf16[512,768]{1,0:T(8,128)(2,1)S(1)}, u32[]{:S(2)}, u32[]{:S(2)}) collective-permute-start(bf16[512,768]{1,0:T(8,128)(2,1)S(1)} %pad_maximum_fusion.1), channel_id=1, source_target_pairs={{0,1},{1,0},{2,3},{3,2},{4,5},{5,4},{6,7},{7,6},{8,9},{9,8},{10,11... | collective-permute-start | bytes 2359304 | tf_op jit(solution)/shard_map/ppermute | solution.py:27
  34.8 2.2 %slice-start = ((s8[4718592]{0:T(1024)(128)(4,1)}), s8[4194304]{0:T(1024)(128)(4,1)S(1)}, s32[]{:S(2)}) async-start(s8[4718592]{0:T(1024)(128)(4,1)} %bitcast.111), calls=%async_computation.1 | async-start | bytes 8388608
  35.4 1.8 %slice-start.1 = ((s8[4718592]{0:T(1024)(128)(4,1)}), s8[524288]{0:T(1024)(128)(4,1)S(1)}, s32[]{:S(2)}) async-start(s8[4718592]{0:T(1024)(128)(4,1)} %bitcast.111), calls=%async_computation.2 | async-start | bytes 1048576
  37.9 9.2 %collective-permute-start.25 = (bf16[128,1024]{1,0:T(8,128)(2,1)S(1)}, bf16[128,1024]{1,0:T(8,128)(2,1)S(1)}, u32[]{:S(2)}, u32[]{:S(2)}) collective-permute-start(bf16[128,1024]{1,0:T(8,128)(2,1)S(1)} %slice.718), channel_id=1, source_target_pairs={{0,16},{8,24},{16,0},{24,8},{1,17},{9,25},{17,1},{25,9},{2,18},{10... | collective-permute-start | bytes 786440 | tf_op jit(solution)/shard_map/ppermute | solution.py:24
  39.2 9.4 %collective-permute-start.5 = (bf16[128,1024]{1,0:T(8,128)(2,1)S(1)}, bf16[128,1024]{1,0:T(8,128)(2,1)S(1)}, u32[]{:S(2)}, u32[]{:S(2)}) collective-permute-start(bf16[128,1024]{1,0:T(8,128)(2,1)S(1)} %pad_maximum_fusion.4), channel_id=1, source_target_pairs={{0,8},{8,0},{16,24},{24,16},{1,9},{9,1},{17,25},{25,17},{2,10},{10... | collective-permute-start | bytes 786440 | tf_op jit(solution)/shard_map/ppermute | solution.py:24
  41.3 12.8 %collective-permute-start.29 = (bf16[128,1024]{1,0:T(8,128)(2,1)S(1)}, bf16[128,1024]{1,0:T(8,128)(2,1)S(1)}, u32[]{:S(2)}, u32[]{:S(2)}) collective-permute-start(bf16[128,1024]{1,0:T(8,128)(2,1)S(1)} %pad_maximum_fusion.10), channel_id=1, source_target_pairs={{0,8},{8,0},{16,24},{24,16},{1,9},{9,1},{17,25},{25,17},{2,10},{10... | collective-permute-start | bytes 786440 | tf_op jit(solution)/shard_map/ppermute | solution.py:24
  42.7 12.9 %collective-permute-start.9 = (bf16[128,1024]{1,0:T(8,128)(2,1)S(1)}, bf16[128,1024]{1,0:T(8,128)(2,1)S(1)}, u32[]{:S(2)}, u32[]{:S(2)}) collective-permute-start(bf16[128,1024]{1,0:T(8,128)(2,1)S(1)} %slice.719), channel_id=1, source_target_pairs={{0,16},{8,24},{16,0},{24,8},{1,17},{9,25},{17,1},{25,9},{2,18},{10... | collective-permute-start | bytes 786440 | tf_op jit(solution)/shard_map/ppermute | solution.py:24
  44.2 41.7 %slice-start.2 = ((s8[9437184]{0:T(1024)(128)(4,1)}), s8[1048576]{0:T(1024)(128)(4,1)S(1)}, s32[]{:S(2)}) async-start(s8[9437184]{0:T(1024)(128)(4,1)} %bitcast.126), calls=%async_computation.3 | async-start | bytes 2097152
  44.8 41.1 %slice-start.3 = ((s8[9437184]{0:T(1024)(128)(4,1)}), s8[4194304]{0:T(1024)(128)(4,1)S(1)}, s32[]{:S(2)}) async-start(s8[9437184]{0:T(1024)(128)(4,1)} %bitcast.126), calls=%async_computation.4 | async-start | bytes 8388608
  44.8 13.5 %collective-permute-start.33 = (bf16[128,1024]{1,0:T(8,128)(2,1)S(1)}, bf16[128,1024]{1,0:T(8,128)(2,1)S(1)}, u32[]{:S(2)}, u32[]{:S(2)}) collective-permute-start(bf16[128,1024]{1,0:T(8,128)(2,1)S(1)} %slice.717), channel_id=1, source_target_pairs={{0,16},{8,24},{16,0},{24,8},{1,17},{9,25},{17,1},{25,9},{2,18},{10... | collective-permute-start | bytes 786440 | tf_op jit(solution)/shard_map/ppermute | solution.py:24
  47.1 12.7 %collective-permute-start.13 = (bf16[128,1024]{1,0:T(8,128)(2,1)S(1)}, bf16[128,1024]{1,0:T(8,128)(2,1)S(1)}, u32[]{:S(2)}, u32[]{:S(2)}) collective-permute-start(bf16[128,1024]{1,0:T(8,128)(2,1)S(1)} %pad_maximum_fusion.7), channel_id=1, source_target_pairs={{0,8},{8,0},{16,24},{24,16},{1,9},{9,1},{17,25},{25,17},{2,10},{10... | collective-permute-start | bytes 786440 | tf_op jit(solution)/shard_map/ppermute | solution.py:24
  48.6 13.9 %collective-permute-start.26 = (bf16[64,1024]{1,0:T(8,128)(2,1)S(1)}, bf16[64,1024]{1,0:T(8,128)(2,1)S(1)}, u32[]{:S(2)}, u32[]{:S(2)}) collective-permute-start(bf16[64,1024]{1,0:T(8,128)(2,1)S(1)} %fusion.130), channel_id=1, source_target_pairs={{0,8},{8,0},{16,24},{24,16},{1,9},{9,1},{17,25},{25,17},{2,10},{10... | collective-permute-start | bytes 393224 | tf_op jit(solution)/shard_map/ppermute | solution.py:24
  54.1 9.8 %collective-permute-start.6 = (bf16[64,1024]{1,0:T(8,128)(2,1)S(1)}, bf16[64,1024]{1,0:T(8,128)(2,1)S(1)}, u32[]{:S(2)}, u32[]{:S(2)}) collective-permute-start(bf16[64,1024]{1,0:T(8,128)(2,1)S(1)} %fusion.139), channel_id=1, source_target_pairs={{0,16},{8,24},{16,0},{24,8},{1,17},{9,25},{17,1},{25,9},{2,18},{10... | collective-permute-start | bytes 393224 | tf_op jit(solution)/shard_map/ppermute | solution.py:24
  55.6 11.1 %collective-permute-start.30 = (bf16[64,1024]{1,0:T(8,128)(2,1)S(1)}, bf16[64,1024]{1,0:T(8,128)(2,1)S(1)}, u32[]{:S(2)}, u32[]{:S(2)}) collective-permute-start(bf16[64,1024]{1,0:T(8,128)(2,1)S(1)} %fusion.127), channel_id=1, source_target_pairs={{0,16},{8,24},{16,0},{24,8},{1,17},{9,25},{17,1},{25,9},{2,18},{10... | collective-permute-start | bytes 393224 | tf_op jit(solution)/shard_map/ppermute | solution.py:24
  58.4 8.3 %collective-permute-start.10 = (bf16[64,1024]{1,0:T(8,128)(2,1)S(1)}, bf16[64,1024]{1,0:T(8,128)(2,1)S(1)}, u32[]{:S(2)}, u32[]{:S(2)}) collective-permute-start(bf16[64,1024]{1,0:T(8,128)(2,1)S(1)} %fusion.136), channel_id=1, source_target_pairs={{0,8},{8,0},{16,24},{24,16},{1,9},{9,1},{17,25},{25,17},{2,10},{10... | collective-permute-start | bytes 393224 | tf_op jit(solution)/shard_map/ppermute | solution.py:24
  59.9 8.6 %collective-permute-start.34 = (bf16[64,1024]{1,0:T(8,128)(2,1)S(1)}, bf16[64,1024]{1,0:T(8,128)(2,1)S(1)}, u32[]{:S(2)}, u32[]{:S(2)}) collective-permute-start(bf16[64,1024]{1,0:T(8,128)(2,1)S(1)} %fusion.124), channel_id=1, source_target_pairs={{0,8},{8,0},{16,24},{24,16},{1,9},{9,1},{17,25},{25,17},{2,10},{10... | collective-permute-start | bytes 393224 | tf_op jit(solution)/shard_map/ppermute | solution.py:24
  62.5 6.0 %collective-permute-start.14 = (bf16[64,1024]{1,0:T(8,128)(2,1)S(1)}, bf16[64,1024]{1,0:T(8,128)(2,1)S(1)}, u32[]{:S(2)}, u32[]{:S(2)}) collective-permute-start(bf16[64,1024]{1,0:T(8,128)(2,1)S(1)} %fusion.133), channel_id=1, source_target_pairs={{0,16},{8,24},{16,0},{24,8},{1,17},{9,25},{17,1},{25,9},{2,18},{10... | collective-permute-start | bytes 393224 | tf_op jit(solution)/shard_map/ppermute | solution.py:24
  63.9 22.0 %slice-start.4 = ((s8[9437184]{0:T(1024)(128)(4,1)}), s8[4194304]{0:T(1024)(128)(4,1)S(1)}, s32[]{:S(2)}) async-start(s8[9437184]{0:T(1024)(128)(4,1)} %bitcast.126), calls=%async_computation.5 | async-start | bytes 8388608
  65.2 8.3 %collective-permute-start.27 = (bf16[64,1024]{1,0:T(8,128)(2,1)S(1)}, bf16[64,1024]{1,0:T(8,128)(2,1)S(1)}, u32[]{:S(2)}, u32[]{:S(2)}) collective-permute-start(bf16[64,1024]{1,0:T(8,128)(2,1)S(1)} %get-tuple-element.59), channel_id=1, source_target_pairs={{0,8},{8,0},{16,24},{24,16},{1,9},{9,1},{17,25},{25,17},{2,10},{10... | collective-permute-start | bytes 393224 | tf_op jit(solution)/shard_map/ppermute | solution.py:24
  67.9 6.4 %collective-permute-start.31 = (bf16[64,1024]{1,0:T(8,128)(2,1)S(1)}, bf16[64,1024]{1,0:T(8,128)(2,1)S(1)}, u32[]{:S(2)}, u32[]{:S(2)}) collective-permute-start(bf16[64,1024]{1,0:T(8,128)(2,1)S(1)} %get-tuple-element.61), channel_id=1, source_target_pairs={{0,16},{8,24},{16,0},{24,8},{1,17},{9,25},{17,1},{25,9},{2,18},{10... | collective-permute-start | bytes 393224 | tf_op jit(solution)/shard_map/ppermute | solution.py:24
  69.9 6.1 %collective-permute-start.35 = (bf16[64,1024]{1,0:T(8,128)(2,1)S(1)}, bf16[64,1024]{1,0:T(8,128)(2,1)S(1)}, u32[]{:S(2)}, u32[]{:S(2)}) collective-permute-start(bf16[64,1024]{1,0:T(8,128)(2,1)S(1)} %get-tuple-element.63), channel_id=1, source_target_pairs={{0,8},{8,0},{16,24},{24,16},{1,9},{9,1},{17,25},{25,17},{2,10},{10... | collective-permute-start | bytes 393224 | tf_op jit(solution)/shard_map/ppermute | solution.py:24
  71.0 6.4 %collective-permute-start.7 = (bf16[64,1024]{1,0:T(8,128)(2,1)S(1)}, bf16[64,1024]{1,0:T(8,128)(2,1)S(1)}, u32[]{:S(2)}, u32[]{:S(2)}) collective-permute-start(bf16[64,1024]{1,0:T(8,128)(2,1)S(1)} %get-tuple-element.58), channel_id=1, source_target_pairs={{0,16},{8,24},{16,0},{24,8},{1,17},{9,25},{17,1},{25,9},{2,18},{10... | collective-permute-start | bytes 393224 | tf_op jit(solution)/shard_map/ppermute | solution.py:24
  72.5 6.4 %collective-permute-start.11 = (bf16[64,1024]{1,0:T(8,128)(2,1)S(1)}, bf16[64,1024]{1,0:T(8,128)(2,1)S(1)}, u32[]{:S(2)}, u32[]{:S(2)}) collective-permute-start(bf16[64,1024]{1,0:T(8,128)(2,1)S(1)} %get-tuple-element.60), channel_id=1, source_target_pairs={{0,8},{8,0},{16,24},{24,16},{1,9},{9,1},{17,25},{25,17},{2,10},{10... | collective-permute-start | bytes 393224 | tf_op jit(solution)/shard_map/ppermute | solution.py:24
  73.5 6.7 %collective-permute-start.15 = (bf16[64,1024]{1,0:T(8,128)(2,1)S(1)}, bf16[64,1024]{1,0:T(8,128)(2,1)S(1)}, u32[]{:S(2)}, u32[]{:S(2)}) collective-permute-start(bf16[64,1024]{1,0:T(8,128)(2,1)S(1)} %get-tuple-element.62), channel_id=1, source_target_pairs={{0,16},{8,24},{16,0},{24,8},{1,17},{9,25},{17,1},{25,9},{2,18},{10... | collective-permute-start | bytes 393224 | tf_op jit(solution)/shard_map/ppermute | solution.py:24
  74.3 18.0 %collective-permute-start.28 = (bf16[128,1024]{1,0:T(8,128)(2,1)S(1)}, bf16[128,1024]{1,0:T(8,128)(2,1)S(1)}, u32[]{:S(2)}, u32[]{:S(2)}) collective-permute-start(bf16[128,1024]{1,0:T(8,128)(2,1)S(1)} %pad_maximum_fusion.9), channel_id=1, source_target_pairs={{0,16},{8,24},{16,0},{24,8},{1,17},{9,25},{17,1},{25,9},{2,18},{10... | collective-permute-start | bytes 786440 | tf_op jit(solution)/shard_map/ppermute | solution.py:24
  76.0 9.2 %collective-permute-start.32 = (bf16[128,1024]{1,0:T(8,128)(2,1)S(1)}, bf16[128,1024]{1,0:T(8,128)(2,1)S(1)}, u32[]{:S(2)}, u32[]{:S(2)}) collective-permute-start(bf16[128,1024]{1,0:T(8,128)(2,1)S(1)} %pad_maximum_fusion.11), channel_id=1, source_target_pairs={{0,8},{8,0},{16,24},{24,16},{1,9},{9,1},{17,25},{25,17},{2,10},{10... | collective-permute-start | bytes 786440 | tf_op jit(solution)/shard_map/ppermute | solution.py:24
  77.3 14.0 %collective-permute-start.36 = (bf16[128,1024]{1,0:T(8,128)(2,1)S(1)}, bf16[128,1024]{1,0:T(8,128)(2,1)S(1)}, u32[]{:S(2)}, u32[]{:S(2)}) collective-permute-start(bf16[128,1024]{1,0:T(8,128)(2,1)S(1)} %pad_maximum_fusion.12), channel_id=1, source_target_pairs={{0,16},{8,24},{16,0},{24,8},{1,17},{9,25},{17,1},{25,9},{2,18},{10... | collective-permute-start | bytes 786440 | tf_op jit(solution)/shard_map/ppermute | solution.py:24
  78.9 17.1 %collective-permute-start.8 = (bf16[128,1024]{1,0:T(8,128)(2,1)S(1)}, bf16[128,1024]{1,0:T(8,128)(2,1)S(1)}, u32[]{:S(2)}, u32[]{:S(2)}) collective-permute-start(bf16[128,1024]{1,0:T(8,128)(2,1)S(1)} %pad_maximum_fusion.5), channel_id=1, source_target_pairs={{0,8},{8,0},{16,24},{24,16},{1,9},{9,1},{17,25},{25,17},{2,10},{10... | collective-permute-start | bytes 786440 | tf_op jit(solution)/shard_map/ppermute | solution.py:24
  80.1 14.8 %collective-permute-start.12 = (bf16[128,1024]{1,0:T(8,128)(2,1)S(1)}, bf16[128,1024]{1,0:T(8,128)(2,1)S(1)}, u32[]{:S(2)}, u32[]{:S(2)}) collective-permute-start(bf16[128,1024]{1,0:T(8,128)(2,1)S(1)} %pad_maximum_fusion.6), channel_id=1, source_target_pairs={{0,16},{8,24},{16,0},{24,8},{1,17},{9,25},{17,1},{25,9},{2,18},{10... | collective-permute-start | bytes 786440 | tf_op jit(solution)/shard_map/ppermute | solution.py:24
  85.2 10.8 %collective-permute-start.16 = (bf16[128,1024]{1,0:T(8,128)(2,1)S(1)}, bf16[128,1024]{1,0:T(8,128)(2,1)S(1)}, u32[]{:S(2)}, u32[]{:S(2)}) collective-permute-start(bf16[128,1024]{1,0:T(8,128)(2,1)S(1)} %pad_maximum_fusion.8), channel_id=1, source_target_pairs={{0,8},{8,0},{16,24},{24,16},{1,9},{9,1},{17,25},{25,17},{2,10},{10... | collective-permute-start | bytes 786440 | tf_op jit(solution)/shard_map/ppermute | solution.py:24
  93.5 4.7 %collective-permute-start.37 = (bf16[256,768]{1,0:T(8,128)(2,1)S(1)}, bf16[256,768]{1,0:T(8,128)(2,1)S(1)}, u32[]{:S(2)}, u32[]{:S(2)}) collective-permute-start(bf16[256,768]{1,0:T(8,128)(2,1)S(1)} %select_convert_fusion), channel_id=1, source_target_pairs={{0,1},{1,0},{2,3},{3,2},{4,5},{5,4},{6,7},{7,6},{8,9},{9,8},{10,11... | collective-permute-start | bytes 1179656 | tf_op jit(solution)/shard_map/ppermute | solution.py:27
  98.1 3.8 %collective-permute-start.17 = (bf16[256,768]{1,0:T(8,128)(2,1)S(1)}, bf16[256,768]{1,0:T(8,128)(2,1)S(1)}, u32[]{:S(2)}, u32[]{:S(2)}) collective-permute-start(bf16[256,768]{1,0:T(8,128)(2,1)S(1)} %select_convert_fusion.1), channel_id=1, source_target_pairs={{0,1},{1,0},{2,3},{3,2},{4,5},{5,4},{6,7},{7,6},{8,9},{9,8},{10,11... | collective-permute-start | bytes 1179656 | tf_op jit(solution)/shard_map/ppermute | solution.py:27
  98.3 5.8 %collective-permute-start.38 = (bf16[64,768]{1,0:T(8,128)(2,1)S(1)}, bf16[64,768]{1,0:T(8,128)(2,1)S(1)}, u32[]{:S(2)}, u32[]{:S(2)}) collective-permute-start(bf16[64,768]{1,0:T(8,128)(2,1)S(1)} %get-tuple-element.48), channel_id=1, source_target_pairs={{0,8},{8,0},{16,24},{24,16},{1,9},{9,1},{17,25},{25,17},{2,10},{10... | collective-permute-start | bytes 294920 | tf_op jit(solution)/shard_map/ppermute | solution.py:24
  99.1 6.5 %collective-permute-start.39 = (bf16[64,768]{1,0:T(8,128)(2,1)S(1)}, bf16[64,768]{1,0:T(8,128)(2,1)S(1)}, u32[]{:S(2)}, u32[]{:S(2)}) collective-permute-start(bf16[64,768]{1,0:T(8,128)(2,1)S(1)} %get-tuple-element.47), channel_id=1, source_target_pairs={{0,16},{8,24},{16,0},{24,8},{1,17},{9,25},{17,1},{25,9},{2,18},{10... | collective-permute-start | bytes 294920 | tf_op jit(solution)/shard_map/ppermute | solution.py:24
  100.4 22.5 %copy-start.1 = (bf16[128,768]{1,0:T(8,128)(2,1)S(1)}, bf16[128,768]{1,0:T(8,128)(2,1)}, u32[]{:S(2)}) copy-start(bf16[128,768]{1,0:T(8,128)(2,1)} %param.5) | copy-start | bytes 589828
  100.4 6.6 %collective-permute-start.40 = (bf16[64,768]{1,0:T(8,128)(2,1)S(1)}, bf16[64,768]{1,0:T(8,128)(2,1)S(1)}, u32[]{:S(2)}, u32[]{:S(2)}) collective-permute-start(bf16[64,768]{1,0:T(8,128)(2,1)S(1)} %get-tuple-element.46), channel_id=1, source_target_pairs={{0,24},{8,16},{16,8},{24,0},{1,25},{9,17},{17,9},{25,1},{2,26},{10... | collective-permute-start | bytes 294920 | tf_op jit(solution)/shard_map/ppermute | solution.py:24
  102.1 8.8 %collective-permute-start.18 = (bf16[64,768]{1,0:T(8,128)(2,1)S(1)}, bf16[64,768]{1,0:T(8,128)(2,1)S(1)}, u32[]{:S(2)}, u32[]{:S(2)}) collective-permute-start(bf16[64,768]{1,0:T(8,128)(2,1)S(1)} %get-tuple-element.38), channel_id=1, source_target_pairs={{0,8},{8,0},{16,24},{24,16},{1,9},{9,1},{17,25},{25,17},{2,10},{10... | collective-permute-start | bytes 294920 | tf_op jit(solution)/shard_map/ppermute | solution.py:24
  102.9 8.0 %collective-permute-start.19 = (bf16[64,768]{1,0:T(8,128)(2,1)S(1)}, bf16[64,768]{1,0:T(8,128)(2,1)S(1)}, u32[]{:S(2)}, u32[]{:S(2)}) collective-permute-start(bf16[64,768]{1,0:T(8,128)(2,1)S(1)} %get-tuple-element.37), channel_id=1, source_target_pairs={{0,16},{8,24},{16,0},{24,8},{1,17},{9,25},{17,1},{25,9},{2,18},{10... | collective-permute-start | bytes 294920 | tf_op jit(solution)/shard_map/ppermute | solution.py:24
  104.1 6.8 %collective-permute-start.20 = (bf16[64,768]{1,0:T(8,128)(2,1)S(1)}, bf16[64,768]{1,0:T(8,128)(2,1)S(1)}, u32[]{:S(2)}, u32[]{:S(2)}) collective-permute-start(bf16[64,768]{1,0:T(8,128)(2,1)S(1)} %get-tuple-element.36), channel_id=1, source_target_pairs={{0,24},{8,16},{16,8},{24,0},{1,25},{9,17},{17,9},{25,1},{2,26},{10... | collective-permute-start | bytes 294920 | tf_op jit(solution)/shard_map/ppermute | solution.py:24
  107.0 7.9 %collective-permute-start.41 = (bf16[32,768]{1,0:T(8,128)(2,1)S(1)}, bf16[32,768]{1,0:T(8,128)(2,1)S(1)}, u32[]{:S(2)}, u32[]{:S(2)}) collective-permute-start(bf16[32,768]{1,0:T(8,128)(2,1)S(1)} %get-tuple-element.41), channel_id=1, source_target_pairs={{0,2},{1,3},{2,4},{3,5},{4,6},{5,7},{6,0},{7,1},{8,10},{9,11},{10,... | collective-permute-start | bytes 147464 | tf_op jit(solution)/shard_map/ppermute | solution.py:30
  107.6 7.3 %collective-permute-start.43 = (bf16[32,768]{1,0:T(8,128)(2,1)S(1)}, bf16[32,768]{1,0:T(8,128)(2,1)S(1)}, u32[]{:S(2)}, u32[]{:S(2)}) collective-permute-start(bf16[32,768]{1,0:T(8,128)(2,1)S(1)} %get-tuple-element.43), channel_id=1, source_target_pairs={{0,6},{1,7},{2,0},{3,1},{4,2},{5,3},{6,4},{7,5},{8,14},{9,15},{10,... | collective-permute-start | bytes 147464 | tf_op jit(solution)/shard_map/ppermute | solution.py:30
  111.0 7.9 %collective-permute-start.21 = (bf16[32,768]{1,0:T(8,128)(2,1)S(1)}, bf16[32,768]{1,0:T(8,128)(2,1)S(1)}, u32[]{:S(2)}, u32[]{:S(2)}) collective-permute-start(bf16[32,768]{1,0:T(8,128)(2,1)S(1)} %get-tuple-element.31), channel_id=1, source_target_pairs={{0,2},{1,3},{2,4},{3,5},{4,6},{5,7},{6,0},{7,1},{8,10},{9,11},{10,... | collective-permute-start | bytes 147464 | tf_op jit(solution)/shard_map/ppermute | solution.py:30
  111.1 7.8 %collective-permute-start.23 = (bf16[32,768]{1,0:T(8,128)(2,1)S(1)}, bf16[32,768]{1,0:T(8,128)(2,1)S(1)}, u32[]{:S(2)}, u32[]{:S(2)}) collective-permute-start(bf16[32,768]{1,0:T(8,128)(2,1)S(1)} %get-tuple-element.33), channel_id=1, source_target_pairs={{0,6},{1,7},{2,0},{3,1},{4,2},{5,3},{6,4},{7,5},{8,14},{9,15},{10,... | collective-permute-start | bytes 147464 | tf_op jit(solution)/shard_map/ppermute | solution.py:30
  114.9 8.0 %collective-permute-start.42 = (bf16[64,768]{1,0:T(8,128)(2,1)S(1)}, bf16[64,768]{1,0:T(8,128)(2,1)S(1)}, u32[]{:S(2)}, u32[]{:S(2)}) collective-permute-start(bf16[64,768]{1,0:T(8,128)(2,1)S(1)} %pad_maximum_fusion.16), channel_id=1, source_target_pairs={{0,2},{1,3},{2,4},{3,5},{4,6},{5,7},{6,0},{7,1},{8,10},{9,11},{10,... | collective-permute-start | bytes 294920 | tf_op jit(solution)/shard_map/ppermute | solution.py:30
  115.0 7.9 %collective-permute-start.44 = (bf16[64,768]{1,0:T(8,128)(2,1)S(1)}, bf16[64,768]{1,0:T(8,128)(2,1)S(1)}, u32[]{:S(2)}, u32[]{:S(2)}) collective-permute-start(bf16[64,768]{1,0:T(8,128)(2,1)S(1)} %pad_maximum_fusion.17), channel_id=1, source_target_pairs={{0,6},{1,7},{2,0},{3,1},{4,2},{5,3},{6,4},{7,5},{8,14},{9,15},{10,... | collective-permute-start | bytes 294920 | tf_op jit(solution)/shard_map/ppermute | solution.py:30
  118.9 6.8 %collective-permute-start.22 = (bf16[64,768]{1,0:T(8,128)(2,1)S(1)}, bf16[64,768]{1,0:T(8,128)(2,1)S(1)}, u32[]{:S(2)}, u32[]{:S(2)}) collective-permute-start(bf16[64,768]{1,0:T(8,128)(2,1)S(1)} %pad_maximum_fusion.14), channel_id=1, source_target_pairs={{0,2},{1,3},{2,4},{3,5},{4,6},{5,7},{6,0},{7,1},{8,10},{9,11},{10,... | collective-permute-start | bytes 294920 | tf_op jit(solution)/shard_map/ppermute | solution.py:30
  119.0 6.7 %collective-permute-start.24 = (bf16[64,768]{1,0:T(8,128)(2,1)S(1)}, bf16[64,768]{1,0:T(8,128)(2,1)S(1)}, u32[]{:S(2)}, u32[]{:S(2)}) collective-permute-start(bf16[64,768]{1,0:T(8,128)(2,1)S(1)} %pad_maximum_fusion.15), channel_id=1, source_target_pairs={{0,6},{1,7},{2,0},{3,1},{4,2},{5,3},{6,4},{7,5},{8,14},{9,15},{10,... | collective-permute-start | bytes 294920 | tf_op jit(solution)/shard_map/ppermute | solution.py:30

commit v2 on v1

--- a/solution.py
+++ b/solution.py
@@ -7,7 +7,7 @@
 floor_value = 0.1
 CORES = 2
 TOKEN_CHUNKS = 2
-COLUMN_CHUNKS = 3
+COLUMN_CHUNKS = 4
 HALVES = True
 
 
@@ -26,9 +26,6 @@
     def over_cores(value):
         return lax.ppermute(value, "mp", [(i, i ^ 1) for i in range(mp)])
 
-    def over_depth(value, shift):
-        return lax.ppermute(value, "mp", [(i, (i + CORES * shift) % mp) for i in range(mp)])
-
     def spread(value, j):
         pairs = []
         for r in range(rows):
@@ -39,22 +36,14 @@
         return lax.ppermute(value, ("rows", "mp"), pairs)
 
     def scatter_depth(parts):
-        half = parts[0].shape[0] // 2
-        middle = parts[depth // 2]
-        up = down = None
-        for distance in range(depth // 2, 0, -1):
-            if distance == depth // 2:
-                give_up, give_down = middle[:half], middle[half:]
-            else:
-                mine_up, mine_down = parts[depth - distance], parts[distance]
-                if distance == depth // 2 - 1:
-                    give_up = jnp.concatenate([mine_up[:half] + up, mine_up[half:]], axis=0)
-                    give_down = jnp.concatenate([mine_down[:half], mine_down[half:] + down], axis=0)
-                else:
-                    give_up, give_down = mine_up + up, mine_down + down
-            up = over_depth(give_up.astype(jnp.bfloat16), 1).astype(jnp.float32)
-            down = over_depth(give_down.astype(jnp.bfloat16), -1).astype(jnp.float32)
-        return parts[0] + up + down
+        size = parts[0].shape[0]
+        held = dict(enumerate(parts))
+        for bit in [1 << n for n in range(depth.bit_length() - 1)]:
+            going = [b for b in held if b & bit]
+            sent = jnp.concatenate([held[b].astype(jnp.bfloat16) for b in going], axis=0)
+            sent = lax.ppermute(sent, "mp", [(i, i ^ (CORES * bit)) for i in range(mp)])
+            held = {b ^ bit: held[b ^ bit] + sent[k * size : (k + 1) * size].astype(jnp.float32) for k, b in enumerate(going)}
+        return held[0]
 
     def body(tokens, norm_gain, hidden_bias, weight_in, weight_out):
         count, width = tokens.shape
@@ -108,10 +97,10 @@
             x_all = [jnp.concatenate(columns, axis=1).reshape(rows, count, features // rows)]
             w_all = [weight_in]
 
-        rows_here = count // TOKEN_CHUNKS
         cols_here = hidden_width // COLUMN_CHUNKS
         results = []
         for t in range(TOKEN_CHUNKS):
+            rows_here = count // TOKEN_CHUNKS
             span = slice(t * rows_here, (t + 1) * rows_here)
             terms = 0.0
             for c in range(COLUMN_CHUNKS):
@@ -153,7 +142,7 @@
             blocks = jnp.moveaxis(blocks, 2, 1).reshape(depth, rows_here, width)
             parts = []
             for j in range(depth):
-                target = (chip - j) % depth
+                target = chip ^ j
                 index = ((target // per_row) ^ row) * per_row + target % per_row
                 parts.append(lax.dynamic_index_in_dim(blocks, index, 0, keepdims=False).astype(jnp.float32))
             results.append((as_float[span] + scatter_depth(parts)).astype(jnp.bfloat16))

time: 127 us -> 128 us (level)
  waiting for transfers between devices: 27.3 us -> 32.6 us
  starting transfers between devices: 65.7 us -> 61.5 us
    ppermute x8 -> x4, starting transfers between devices: 15.6 us -> 4.86 us  [scatter_depth(): sent = lax.ppermute(sent, 'mp', [(i, i ^ CORES * bit) for i in range(mp)])]
    ppermute x8 -> x4, waiting for transfers between devices: 2.79 us -> 9.79 us  [scatter_depth(): sent = lax.ppermute(sent, 'mp', [(i, i ^ CORES * bit) for i in range(mp)])]
    ppermute x30 -> x38, starting transfers between devices: 33.9 us -> 40.3 us  [over_rows(): return lax.ppermute(value, 'rows', [(i, i ^ flip) for i in range(rows)])]
    ppermute x30 -> x38, waiting for transfers between devices: 20.8 us -> 19.2 us  [over_rows(): return lax.ppermute(value, 'rows', [(i, i ^ flip) for i in range(rows)])]
    dot_general x12 -> x16, matrix products: 7.08 us -> 7.64 us  [body(): part = part + jnp.dot(x, w[:, cols], preferred_element_type=jnp.float32)]
    dot_general x6 -> x8, matrix products: 5.98 us -> 6.36 us  [body(): jnp.dot(block, weight_out[cols], preferred_element_type=jnp.float32)]
    convert_element_type x3 -> x4, other arithmetic: 3.82 us -> 3.83 us  [body(): jax.nn.gelu(held[0] + hidden_bias[None, cols], approximate=False)]
  transfers between devices with their start and end apart: 46 -> 50, of which waited for: 14 -> 17; matrix products, arithmetic and copies ran while one was open for 23% -> 23% of each run, Pallas kernels for 0% -> 0%
where the time goes in v2:
time: 128 us
  starting transfers between devices  61.5 us (48%)
  waiting for transfers between devices  32.6 us (25%)
  matrix products  14 us (11%)
  local copies, waits for them, and re-layouts  12 us (9%)
  other arithmetic  7.12 us (6%)
    ppermute x38, starting transfers between devices, over_rows(): return lax.ppermute(value, 'rows', [(i, i ^ flip) for i in range(rows)])  40.3 us
    ppermute x38, waiting for transfers between devices, over_rows(): return lax.ppermute(value, 'rows', [(i, i ^ flip) for i in range(rows)])  19.2 us
    ppermute x4, starting transfers between devices, spread(): return lax.ppermute(value, ('rows', 'mp'), pairs)  11.8 us
    ppermute x4, waiting for transfers between devices, scatter_depth(): sent = lax.ppermute(sent, 'mp', [(i, i ^ CORES * bit) for i in range(mp)])  9.79 us
    reshape x1, local copies, waits for them, and re-layouts, body(): lax.dynamic_index_in_dim(blocks_in, 1 - core, 1, keepdims=False)  8.32 us
    dot_general x16, matrix products, body(): part = part + jnp.dot(x, w[:, cols], preferred_element_type=jnp.float32)  7.64 us
    dot_general x8, matrix products, body(): jnp.dot(block, weight_out[cols], preferred_element_type=jnp.float32)  6.36 us
    ppermute x4, starting transfers between devices, scatter_depth(): sent = lax.ppermute(sent, 'mp', [(i, i ^ CORES * bit) for i in range(mp)])  4.86 us
  transfers between devices with their start and end apart: 50, of which 17 were waited for; matrix products, arithmetic and copies ran while one was open for 23% of the time, Pallas kernels for 0%

profile of v2, /device:TPU:0, one launch (start us, length us, event | category | flops | bytes accessed | tf_op | source)
XLA Modules:
  0.0 128.1 jit_solution(5337967399818419895)
XLA Ops:
  0.0 1.6 %collective-permute-start = (bf16[128,768]{1,0:T(8,128)(2,1)}, bf16[128,768]{1,0:T(8,128)(2,1)S(1)}, u32[]{:S(2)}, u32[]{:S(2)}) collective-permute-start(bf16[128,768]{1,0:T(8,128)(2,1)} %param.5), channel_id=1, source_target_pairs={{0,0},{1,1},{2,8},{3,9},{4,16},{5,17},{6,24},{7,25},{8,2},{9,3},{1... | collective-permute-start | bytes 589832 | tf_op jit(solution)/shard_map/ppermute | solution.py:36
  1.6 4.8 %collective-permute-start.1 = (bf16[128,768]{1,0:T(8,128)(2,1)}, bf16[128,768]{1,0:T(8,128)(2,1)S(1)}, u32[]{:S(2)}, u32[]{:S(2)}) collective-permute-start(bf16[128,768]{1,0:T(8,128)(2,1)} %param.5), channel_id=1, source_target_pairs={{0,2},{1,3},{2,10},{3,11},{4,18},{5,19},{6,26},{7,27},{8,0},{9,1},... | collective-permute-start | bytes 589832 | tf_op jit(solution)/shard_map/ppermute | solution.py:36
  6.4 3.5 %collective-permute-start.2 = (bf16[128,768]{1,0:T(8,128)(2,1)}, bf16[128,768]{1,0:T(8,128)(2,1)S(1)}, u32[]{:S(2)}, u32[]{:S(2)}) collective-permute-start(bf16[128,768]{1,0:T(8,128)(2,1)} %param.5), channel_id=1, source_target_pairs={{0,4},{1,5},{2,12},{3,13},{4,20},{5,21},{6,28},{7,29},{8,6},{9,7},... | collective-permute-start | bytes 589832 | tf_op jit(solution)/shard_map/ppermute | solution.py:36
  9.9 1.9 %collective-permute-start.3 = (bf16[128,768]{1,0:T(8,128)(2,1)}, bf16[128,768]{1,0:T(8,128)(2,1)S(1)}, u32[]{:S(2)}, u32[]{:S(2)}) collective-permute-start(bf16[128,768]{1,0:T(8,128)(2,1)} %param.5), channel_id=1, source_target_pairs={{0,6},{1,7},{2,14},{3,15},{4,22},{5,23},{6,30},{7,31},{8,4},{9,5},... | collective-permute-start | bytes 589832 | tf_op jit(solution)/shard_map/ppermute | solution.py:36
  11.8 1.1 convert_reduce_fusion
  13.5 4.2 %all-to-all-start = ((f32[32,2,128]{2,1,0:T(2,128)}), f32[32,2,128]{2,1,0:T(2,128)S(1)}, u32[]{:S(2)}, u32[]{:S(2)}) async-start(f32[32,2,128]{2,1,0:T(2,128)} %broadcast_in_dim.2), calls=%async_computation | async-start | bytes 65536 | tf_op jit(solution)/shard_map/all_to_all | solution.py:58
  17.8 8.3 %dynamic-slice_bitcast_fusion = (bf16[768,3072]{1,0:T(8,128)(2,1)}, bf16[768,3072]{1,0:T(8,128)(2,1)}) fusion(bf16[1,2,768,3072]{3,2,1,0:T(8,128)(2,1)} %bitcast.111, s32[]{:T(128)S(6)} %select_n.121, s32[]{:T(128)S(6)} %select_n.117), kind=kLoop, calls=%fused_computation | loop fusion | bytes 18874376 | tf_op jit(solution)/shard_map/reshape | solution.py:87
  26.2 0.8 dynamic_slice.70
  27.0 3.6 %all-to-all-done = f32[32,2,128]{2,1,0:T(2,128)S(1)} async-done(((f32[32,2,128]{2,1,0:T(2,128)}), f32[32,2,128]{2,1,0:T(2,128)S(1)}, u32[]{:S(2)}, u32[]{:S(2)}) %all-to-all-start) | async-done | bytes 32800 | tf_op jit(solution)/shard_map/all_to_all | solution.py:58
  31.4 1.7 %copy-done = bf16[768,3072]{1,0:T(8,128)(2,1)S(1)} copy-done((bf16[768,3072]{1,0:T(8,128)(2,1)S(1)}, bf16[768,3072]{1,0:T(8,128)(2,1)}, u32[]{:S(2)}) %copy-start) | copy-done | bytes 4718616
  38.9 1.4 %collective-permute-start.5 = (bf16[128,768]{1,0:T(8,128)(2,1)S(1)}, bf16[128,768]{1,0:T(8,128)(2,1)S(1)}, u32[]{:S(2)}, u32[]{:S(2)}) collective-permute-start(bf16[128,768]{1,0:T(8,128)(2,1)S(1)} %pad_maximum_fusion.4), channel_id=1, source_target_pairs={{0,8},{8,0},{16,24},{24,16},{1,9},{9,1},{17,25},{25,17},{2,10},{10... | collective-permute-start | bytes 589832 | tf_op jit(solution)/shard_map/ppermute | solution.py:24
  42.1 1.5 %collective-permute-start.9 = (bf16[128,768]{1,0:T(8,128)(2,1)S(1)}, bf16[128,768]{1,0:T(8,128)(2,1)S(1)}, u32[]{:S(2)}, u32[]{:S(2)}) collective-permute-start(bf16[128,768]{1,0:T(8,128)(2,1)S(1)} %slice.751), channel_id=1, source_target_pairs={{0,16},{8,24},{16,0},{24,8},{1,17},{9,25},{17,1},{25,9},{2,18},{10... | collective-permute-start | bytes 589832 | tf_op jit(solution)/shard_map/ppermute | solution.py:24
  46.4 1.5 %collective-permute-start.13 = (bf16[128,768]{1,0:T(8,128)(2,1)S(1)}, bf16[128,768]{1,0:T(8,128)(2,1)S(1)}, u32[]{:S(2)}, u32[]{:S(2)}) collective-permute-start(bf16[128,768]{1,0:T(8,128)(2,1)S(1)} %pad_maximum_fusion.7), channel_id=1, source_target_pairs={{0,8},{8,0},{16,24},{24,16},{1,9},{9,1},{17,25},{25,17},{2,10},{10... | collective-permute-start | bytes 589832 | tf_op jit(solution)/shard_map/ppermute | solution.py:24
  47.8 2.1 %collective-permute-done.9 = bf16[128,768]{1,0:T(8,128)(2,1)S(1)} collective-permute-done((bf16[128,768]{1,0:T(8,128)(2,1)S(1)}, bf16[128,768]{1,0:T(8,128)(2,1)S(1)}, u32[]{:S(2)}, u32[]{:S(2)}) %collective-permute-start.9) | collective-permute-done | bytes 196640 | tf_op jit(solution)/shard_map/ppermute | solution.py:24
  49.9 1.4 %collective-permute-start.39 = (bf16[128,768]{1,0:T(8,128)(2,1)S(1)}, bf16[128,768]{1,0:T(8,128)(2,1)S(1)}, u32[]{:S(2)}, u32[]{:S(2)}) collective-permute-start(bf16[128,768]{1,0:T(8,128)(2,1)S(1)} %pad_maximum_fusion.15), channel_id=1, source_target_pairs={{0,8},{8,0},{16,24},{24,16},{1,9},{9,1},{17,25},{25,17},{2,10},{10... | collective-permute-start | bytes 589832 | tf_op jit(solution)/shard_map/ppermute | solution.py:24
  51.3 1.8 %collective-permute-done.35 = bf16[128,768]{1,0:T(8,128)(2,1)S(1)} collective-permute-done((bf16[128,768]{1,0:T(8,128)(2,1)S(1)}, bf16[128,768]{1,0:T(8,128)(2,1)S(1)}, u32[]{:S(2)}, u32[]{:S(2)}) %collective-permute-start.35) | collective-permute-done | bytes 196640 | tf_op jit(solution)/shard_map/ppermute | solution.py:24
  53.1 0.8 collective-permute-start.17
  53.9 1.5 %collective-permute-start.28 = (bf16[64,768]{1,0:T(8,128)(2,1)S(1)}, bf16[64,768]{1,0:T(8,128)(2,1)S(1)}, u32[]{:S(2)}, u32[]{:S(2)}) collective-permute-start(bf16[64,768]{1,0:T(8,128)(2,1)S(1)} %fusion.135), channel_id=1, source_target_pairs={{0,8},{8,0},{16,24},{24,16},{1,9},{9,1},{17,25},{25,17},{2,10},{10... | collective-permute-start | bytes 294920 | tf_op jit(solution)/shard_map/ppermute | solution.py:24
  55.4 1.3 %collective-permute-start.6 = (bf16[64,768]{1,0:T(8,128)(2,1)S(1)}, bf16[64,768]{1,0:T(8,128)(2,1)S(1)}, u32[]{:S(2)}, u32[]{:S(2)}) collective-permute-start(bf16[64,768]{1,0:T(8,128)(2,1)S(1)} %fusion.148), channel_id=1, source_target_pairs={{0,16},{8,24},{16,0},{24,8},{1,17},{9,25},{17,1},{25,9},{2,18},{10... | collective-permute-start | bytes 294920 | tf_op jit(solution)/shard_map/ppermute | solution.py:24
  56.7 3.5 %collective-permute-done.17 = bf16[128,768]{1,0:T(8,128)(2,1)S(1)} collective-permute-done((bf16[128,768]{1,0:T(8,128)(2,1)S(1)}, bf16[128,768]{1,0:T(8,128)(2,1)S(1)}, u32[]{:S(2)}, u32[]{:S(2)}) %collective-permute-start.17) | collective-permute-done | bytes 196640 | tf_op jit(solution)/shard_map/ppermute | solution.py:24
  60.2 0.9 collective-permute-start.32
  61.2 0.9 collective-permute-start.10
  62.1 1.3 %collective-permute-start.36 = (bf16[64,768]{1,0:T(8,128)(2,1)S(1)}, bf16[64,768]{1,0:T(8,128)(2,1)S(1)}, u32[]{:S(2)}, u32[]{:S(2)}) collective-permute-start(bf16[64,768]{1,0:T(8,128)(2,1)S(1)} %fusion.129), channel_id=1, source_target_pairs={{0,8},{8,0},{16,24},{24,16},{1,9},{9,1},{17,25},{25,17},{2,10},{10... | collective-permute-start | bytes 294920 | tf_op jit(solution)/shard_map/ppermute | solution.py:24
  63.4 1.2 collective-permute-start.14
  64.6 0.9 collective-permute-start.40
  65.5 0.9 fusion.104
  66.4 0.9 collective-permute-start.18
  67.3 1.2 collective-permute-start.29
  68.5 0.9 fusion.107
  69.5 1.2 collective-permute-start.33
  70.6 1.1 fusion.110
  71.7 1.5 %collective-permute-start.37 = (bf16[64,768]{1,0:T(8,128)(2,1)S(1)}, bf16[64,768]{1,0:T(8,128)(2,1)S(1)}, u32[]{:S(2)}, u32[]{:S(2)}) collective-permute-start(bf16[64,768]{1,0:T(8,128)(2,1)S(1)} %get-tuple-element.60), channel_id=1, source_target_pairs={{0,8},{8,0},{16,24},{24,16},{1,9},{9,1},{17,25},{25,17},{2,10},{10... | collective-permute-start | bytes 294920 | tf_op jit(solution)/shard_map/ppermute | solution.py:24
  73.2 0.9 fusion.113
  74.5 1.7 %collective-permute-start.7 = (bf16[64,768]{1,0:T(8,128)(2,1)S(1)}, bf16[64,768]{1,0:T(8,128)(2,1)S(1)}, u32[]{:S(2)}, u32[]{:S(2)}) collective-permute-start(bf16[64,768]{1,0:T(8,128)(2,1)S(1)} %get-tuple-element.55), channel_id=1, source_target_pairs={{0,16},{8,24},{16,0},{24,8},{1,17},{9,25},{17,1},{25,9},{2,18},{10... | collective-permute-start | bytes 294920 | tf_op jit(solution)/shard_map/ppermute | solution.py:24
  76.9 1.0 collective-permute-start.15
  77.9 1.0 collective-permute-start.19
  78.9 1.0 collective-permute-done.41
  80.6 1.4 %collective-permute-done.7 = bf16[64,768]{1,0:T(8,128)(2,1)S(1)} collective-permute-done((bf16[64,768]{1,0:T(8,128)(2,1)S(1)}, bf16[64,768]{1,0:T(8,128)(2,1)S(1)}, u32[]{:S(2)}, u32[]{:S(2)}) %collective-permute-start.7) | collective-permute-done | bytes 98336 | tf_op jit(solution)/shard_map/ppermute | solution.py:24
  82.5 1.1 collective-permute-start.38
  84.5 1.7 %collective-permute-start.8 = (bf16[128,768]{1,0:T(8,128)(2,1)S(1)}, bf16[128,768]{1,0:T(8,128)(2,1)S(1)}, u32[]{:S(2)}, u32[]{:S(2)}) collective-permute-start(bf16[128,768]{1,0:T(8,128)(2,1)S(1)} %pad_maximum_fusion.5), channel_id=1, source_target_pairs={{0,8},{8,0},{16,24},{24,16},{1,9},{9,1},{17,25},{25,17},{2,10},{10... | collective-permute-start | bytes 589832 | tf_op jit(solution)/shard_map/ppermute | solution.py:24
  86.2 2.8 %collective-permute-done.34 = bf16[128,768]{1,0:T(8,128)(2,1)S(1)} collective-permute-done((bf16[128,768]{1,0:T(8,128)(2,1)S(1)}, bf16[128,768]{1,0:T(8,128)(2,1)S(1)}, u32[]{:S(2)}, u32[]{:S(2)}) %collective-permute-start.34) | collective-permute-done | bytes 196640 | tf_op jit(solution)/shard_map/ppermute | solution.py:24
  89.1 0.9 collective-permute-start.12
  90.0 1.2 collective-permute-done.42
  91.2 1.4 %collective-permute-start.16 = (bf16[128,768]{1,0:T(8,128)(2,1)S(1)}, bf16[128,768]{1,0:T(8,128)(2,1)S(1)}, u32[]{:S(2)}, u32[]{:S(2)}) collective-permute-start(bf16[128,768]{1,0:T(8,128)(2,1)S(1)} %pad_maximum_fusion.8), channel_id=1, source_target_pairs={{0,8},{8,0},{16,24},{24,16},{1,9},{9,1},{17,25},{25,17},{2,10},{10... | collective-permute-start | bytes 589832 | tf_op jit(solution)/shard_map/ppermute | solution.py:24
  92.6 0.8 collective-permute-start.20
  93.4 0.8 fusion.8
  94.2 0.8 fusion.12
  95.0 0.8 fusion.4
  95.8 0.8 fusion.1
  96.8 0.8 fusion.14
  99.1 0.8 fusion.10
  99.9 0.9 fusion.3
  101.8 1.1 collective-permute-start.45
  102.9 1.8 %collective-permute-start.46 = (bf16[64,768]{1,0:T(8,128)(2,1)S(1)}, bf16[64,768]{1,0:T(8,128)(2,1)S(1)}, u32[]{:S(2)}, u32[]{:S(2)}) collective-permute-start(bf16[64,768]{1,0:T(8,128)(2,1)S(1)} %get-tuple-element.36), channel_id=1, source_target_pairs={{0,24},{8,16},{16,8},{24,0},{1,25},{9,17},{17,9},{25,1},{2,26},{10... | collective-permute-start | bytes 294920 | tf_op jit(solution)/shard_map/ppermute | solution.py:24
  105.5 1.1 collective-permute-start.23
  106.9 1.6 %collective-permute-start.24 = (bf16[64,768]{1,0:T(8,128)(2,1)S(1)}, bf16[64,768]{1,0:T(8,128)(2,1)S(1)}, u32[]{:S(2)}, u32[]{:S(2)}) collective-permute-start(bf16[64,768]{1,0:T(8,128)(2,1)S(1)} %get-tuple-element.26), channel_id=1, source_target_pairs={{0,24},{8,16},{16,8},{24,0},{1,25},{9,17},{17,9},{25,1},{2,26},{10... | collective-permute-start | bytes 294920 | tf_op jit(solution)/shard_map/ppermute | solution.py:24
  108.4 1.0 collective-permute-done.46
  110.2 0.9 collective-permute-done.22
  111.1 1.9 %collective-permute-done.23 = bf16[64,768]{1,0:T(8,128)(2,1)S(1)} collective-permute-done((bf16[64,768]{1,0:T(8,128)(2,1)S(1)}, bf16[64,768]{1,0:T(8,128)(2,1)S(1)}, u32[]{:S(2)}, u32[]{:S(2)}) %collective-permute-start.23) | collective-permute-done | bytes 98336 | tf_op jit(solution)/shard_map/ppermute | solution.py:24
  113.8 1.8 %collective-permute-done.47 = bf16[128,768]{1,0:T(8,128)(2,1)S(1)} collective-permute-done((bf16[128,768]{1,0:T(8,128)(2,1)S(1)}, bf16[128,768]{1,0:T(8,128)(2,1)S(1)}, u32[]{:S(2)}, u32[]{:S(2)}) %collective-permute-start.47) | collective-permute-done | bytes 196640 | tf_op jit(solution)/shard_map/ppermute | solution.py:44
  115.6 2.0 %collective-permute-start.48 = (bf16[64,768]{1,0:T(8,128)(2,1)S(1)}, bf16[64,768]{1,0:T(8,128)(2,1)S(1)}, u32[]{:S(2)}, u32[]{:S(2)}) collective-permute-start(bf16[64,768]{1,0:T(8,128)(2,1)S(1)} %fusion.152), channel_id=1, source_target_pairs={{0,4},{1,5},{2,6},{3,7},{4,0},{5,1},{6,2},{7,3},{8,12},{9,13},{10,... | collective-permute-start | bytes 294920 | tf_op jit(solution)/shard_map/ppermute | solution.py:44
  117.7 3.3 %collective-permute-done.25 = bf16[128,768]{1,0:T(8,128)(2,1)S(1)} collective-permute-done((bf16[128,768]{1,0:T(8,128)(2,1)S(1)}, bf16[128,768]{1,0:T(8,128)(2,1)S(1)}, u32[]{:S(2)}, u32[]{:S(2)}) %collective-permute-start.25) | collective-permute-done | bytes 196640 | tf_op jit(solution)/shard_map/ppermute | solution.py:44
  121.0 1.6 %collective-permute-start.26 = (bf16[64,768]{1,0:T(8,128)(2,1)S(1)}, bf16[64,768]{1,0:T(8,128)(2,1)S(1)}, u32[]{:S(2)}, u32[]{:S(2)}) collective-permute-start(bf16[64,768]{1,0:T(8,128)(2,1)S(1)} %fusion.154), channel_id=1, source_target_pairs={{0,4},{1,5},{2,6},{3,7},{4,0},{5,1},{6,2},{7,3},{8,12},{9,13},{10,... | collective-permute-start | bytes 294920 | tf_op jit(solution)/shard_map/ppermute | solution.py:44
  122.6 4.7 %collective-permute-done.26 = bf16[64,768]{1,0:T(8,128)(2,1)S(1)} collective-permute-done((bf16[64,768]{1,0:T(8,128)(2,1)S(1)}, bf16[64,768]{1,0:T(8,128)(2,1)S(1)}, u32[]{:S(2)}, u32[]{:S(2)}) %collective-permute-start.26) | collective-permute-done | bytes 98336 | tf_op jit(solution)/shard_map/ppermute | solution.py:44
  (149 shorter events, 20.8 us)
Async XLA Ops:
  0.0 30.7 %collective-permute-start = (bf16[128,768]{1,0:T(8,128)(2,1)}, bf16[128,768]{1,0:T(8,128)(2,1)S(1)}, u32[]{:S(2)}, u32[]{:S(2)}) collective-permute-start(bf16[128,768]{1,0:T(8,128)(2,1)} %param.5), channel_id=1, source_target_pairs={{0,0},{1,1},{2,8},{3,9},{4,16},{5,17},{6,24},{7,25},{8,2},{9,3},{1... | collective-permute-start | bytes 589832 | tf_op jit(solution)/shard_map/ppermute | solution.py:36
  1.6 29.1 %collective-permute-start.1 = (bf16[128,768]{1,0:T(8,128)(2,1)}, bf16[128,768]{1,0:T(8,128)(2,1)S(1)}, u32[]{:S(2)}, u32[]{:S(2)}) collective-permute-start(bf16[128,768]{1,0:T(8,128)(2,1)} %param.5), channel_id=1, source_target_pairs={{0,2},{1,3},{2,10},{3,11},{4,18},{5,19},{6,26},{7,27},{8,0},{9,1},... | collective-permute-start | bytes 589832 | tf_op jit(solution)/shard_map/ppermute | solution.py:36
  6.4 24.3 %collective-permute-start.2 = (bf16[128,768]{1,0:T(8,128)(2,1)}, bf16[128,768]{1,0:T(8,128)(2,1)S(1)}, u32[]{:S(2)}, u32[]{:S(2)}) collective-permute-start(bf16[128,768]{1,0:T(8,128)(2,1)} %param.5), channel_id=1, source_target_pairs={{0,4},{1,5},{2,12},{3,13},{4,20},{5,21},{6,28},{7,29},{8,6},{9,7},... | collective-permute-start | bytes 589832 | tf_op jit(solution)/shard_map/ppermute | solution.py:36
  9.9 20.8 %collective-permute-start.3 = (bf16[128,768]{1,0:T(8,128)(2,1)}, bf16[128,768]{1,0:T(8,128)(2,1)S(1)}, u32[]{:S(2)}, u32[]{:S(2)}) collective-permute-start(bf16[128,768]{1,0:T(8,128)(2,1)} %param.5), channel_id=1, source_target_pairs={{0,6},{1,7},{2,14},{3,15},{4,22},{5,23},{6,30},{7,31},{8,4},{9,5},... | collective-permute-start | bytes 589832 | tf_op jit(solution)/shard_map/ppermute | solution.py:36
  13.5 17.0 %all-to-all-start = ((f32[32,2,128]{2,1,0:T(2,128)}), f32[32,2,128]{2,1,0:T(2,128)S(1)}, u32[]{:S(2)}, u32[]{:S(2)}) async-start(f32[32,2,128]{2,1,0:T(2,128)} %broadcast_in_dim.2), calls=%async_computation | async-start | bytes 65536 | tf_op jit(solution)/shard_map/all_to_all | solution.py:58
  17.7 8.3 %copy-start.2 = (f32[3072]{0:T(1024)S(1)}, f32[3072]{0:T(1024)}, u32[]{:S(2)}) copy-start(f32[3072]{0:T(1024)} %param.7) | copy-start | bytes 36868
  30.8 2.3 %copy-start = (bf16[768,3072]{1,0:T(8,128)(2,1)S(1)}, bf16[768,3072]{1,0:T(8,128)(2,1)}, u32[]{:S(2)}) copy-start(bf16[768,3072]{1,0:T(8,128)(2,1)} %get-tuple-element.7) | copy-start | bytes 14155780
  31.2 5.9 %collective-permute-start.4 = (bf16[512,768]{1,0:T(8,128)(2,1)S(1)}, bf16[512,768]{1,0:T(8,128)(2,1)S(1)}, u32[]{:S(2)}, u32[]{:S(2)}) collective-permute-start(bf16[512,768]{1,0:T(8,128)(2,1)S(1)} %pad_maximum_fusion.1), channel_id=1, source_target_pairs={{0,1},{1,0},{2,3},{3,2},{4,5},{5,4},{6,7},{7,6},{8,9},{9,8},{10,11... | collective-permute-start | bytes 2359304 | tf_op jit(solution)/shard_map/ppermute | solution.py:27
  34.6 2.5 %slice-start = ((s8[4718592]{0:T(1024)(128)(4,1)}), s8[4194304]{0:T(1024)(128)(4,1)S(1)}, s32[]{:S(2)}) async-start(s8[4718592]{0:T(1024)(128)(4,1)} %bitcast.93), calls=%async_computation.1 | async-start | bytes 8388608
  35.6 1.6 %slice-start.1 = ((s8[4718592]{0:T(1024)(128)(4,1)}), s8[524288]{0:T(1024)(128)(4,1)S(1)}, s32[]{:S(2)}) async-start(s8[4718592]{0:T(1024)(128)(4,1)} %bitcast.93), calls=%async_computation.2 | async-start | bytes 1048576
  37.7 8.7 %collective-permute-start.27 = (bf16[128,768]{1,0:T(8,128)(2,1)S(1)}, bf16[128,768]{1,0:T(8,128)(2,1)S(1)}, u32[]{:S(2)}, u32[]{:S(2)}) collective-permute-start(bf16[128,768]{1,0:T(8,128)(2,1)S(1)} %slice.749), channel_id=1, source_target_pairs={{0,16},{8,24},{16,0},{24,8},{1,17},{9,25},{17,1},{25,9},{2,18},{10... | collective-permute-start | bytes 589832 | tf_op jit(solution)/shard_map/ppermute | solution.py:24
  38.9 15.0 %collective-permute-start.5 = (bf16[128,768]{1,0:T(8,128)(2,1)S(1)}, bf16[128,768]{1,0:T(8,128)(2,1)S(1)}, u32[]{:S(2)}, u32[]{:S(2)}) collective-permute-start(bf16[128,768]{1,0:T(8,128)(2,1)S(1)} %pad_maximum_fusion.4), channel_id=1, source_target_pairs={{0,8},{8,0},{16,24},{24,16},{1,9},{9,1},{17,25},{25,17},{2,10},{10... | collective-permute-start | bytes 589832 | tf_op jit(solution)/shard_map/ppermute | solution.py:24
  40.8 14.6 %collective-permute-start.31 = (bf16[128,768]{1,0:T(8,128)(2,1)S(1)}, bf16[128,768]{1,0:T(8,128)(2,1)S(1)}, u32[]{:S(2)}, u32[]{:S(2)}) collective-permute-start(bf16[128,768]{1,0:T(8,128)(2,1)S(1)} %pad_maximum_fusion.12), channel_id=1, source_target_pairs={{0,8},{8,0},{16,24},{24,16},{1,9},{9,1},{17,25},{25,17},{2,10},{10... | collective-permute-start | bytes 589832 | tf_op jit(solution)/shard_map/ppermute | solution.py:24
  42.1 7.8 %collective-permute-start.9 = (bf16[128,768]{1,0:T(8,128)(2,1)S(1)}, bf16[128,768]{1,0:T(8,128)(2,1)S(1)}, u32[]{:S(2)}, u32[]{:S(2)}) collective-permute-start(bf16[128,768]{1,0:T(8,128)(2,1)S(1)} %slice.751), channel_id=1, source_target_pairs={{0,16},{8,24},{16,0},{24,8},{1,17},{9,25},{17,1},{25,9},{2,18},{10... | collective-permute-start | bytes 589832 | tf_op jit(solution)/shard_map/ppermute | solution.py:24
  44.1 9.0 %collective-permute-start.35 = (bf16[128,768]{1,0:T(8,128)(2,1)S(1)}, bf16[128,768]{1,0:T(8,128)(2,1)S(1)}, u32[]{:S(2)}, u32[]{:S(2)}) collective-permute-start(bf16[128,768]{1,0:T(8,128)(2,1)S(1)} %slice.748), channel_id=1, source_target_pairs={{0,16},{8,24},{16,0},{24,8},{1,17},{9,25},{17,1},{25,9},{2,18},{10... | collective-permute-start | bytes 589832 | tf_op jit(solution)/shard_map/ppermute | solution.py:24
  44.7 48.7 %slice-start.2 = ((s8[9437184]{0:T(1024)(128)(4,1)}), s8[1048576]{0:T(1024)(128)(4,1)S(1)}, s32[]{:S(2)}) async-start(s8[9437184]{0:T(1024)(128)(4,1)} %bitcast.113), calls=%async_computation.3 | async-start | bytes 2097152
  45.7 47.7 %slice-start.3 = ((s8[9437184]{0:T(1024)(128)(4,1)}), s8[4194304]{0:T(1024)(128)(4,1)S(1)}, s32[]{:S(2)}) async-start(s8[9437184]{0:T(1024)(128)(4,1)} %bitcast.113), calls=%async_computation.4 | async-start | bytes 8388608
  46.4 14.8 %collective-permute-start.13 = (bf16[128,768]{1,0:T(8,128)(2,1)S(1)}, bf16[128,768]{1,0:T(8,128)(2,1)S(1)}, u32[]{:S(2)}, u32[]{:S(2)}) collective-permute-start(bf16[128,768]{1,0:T(8,128)(2,1)S(1)} %pad_maximum_fusion.7), channel_id=1, source_target_pairs={{0,8},{8,0},{16,24},{24,16},{1,9},{9,1},{17,25},{25,17},{2,10},{10... | collective-permute-start | bytes 589832 | tf_op jit(solution)/shard_map/ppermute | solution.py:24
  49.9 12.2 %collective-permute-start.39 = (bf16[128,768]{1,0:T(8,128)(2,1)S(1)}, bf16[128,768]{1,0:T(8,128)(2,1)S(1)}, u32[]{:S(2)}, u32[]{:S(2)}) collective-permute-start(bf16[128,768]{1,0:T(8,128)(2,1)S(1)} %pad_maximum_fusion.15), channel_id=1, source_target_pairs={{0,8},{8,0},{16,24},{24,16},{1,9},{9,1},{17,25},{25,17},{2,10},{10... | collective-permute-start | bytes 589832 | tf_op jit(solution)/shard_map/ppermute | solution.py:24
  53.1 7.2 %collective-permute-start.17 = (bf16[128,768]{1,0:T(8,128)(2,1)S(1)}, bf16[128,768]{1,0:T(8,128)(2,1)S(1)}, u32[]{:S(2)}, u32[]{:S(2)}) collective-permute-start(bf16[128,768]{1,0:T(8,128)(2,1)S(1)} %slice.750), channel_id=1, source_target_pairs={{0,16},{8,24},{16,0},{24,8},{1,17},{9,25},{17,1},{25,9},{2,18},{10... | collective-permute-start | bytes 589832 | tf_op jit(solution)/shard_map/ppermute | solution.py:24
  53.9 9.5 %collective-permute-start.28 = (bf16[64,768]{1,0:T(8,128)(2,1)S(1)}, bf16[64,768]{1,0:T(8,128)(2,1)S(1)}, u32[]{:S(2)}, u32[]{:S(2)}) collective-permute-start(bf16[64,768]{1,0:T(8,128)(2,1)S(1)} %fusion.135), channel_id=1, source_target_pairs={{0,8},{8,0},{16,24},{24,16},{1,9},{9,1},{17,25},{25,17},{2,10},{10... | collective-permute-start | bytes 294920 | tf_op jit(solution)/shard_map/ppermute | solution.py:24
  55.4 9.2 %collective-permute-start.6 = (bf16[64,768]{1,0:T(8,128)(2,1)S(1)}, bf16[64,768]{1,0:T(8,128)(2,1)S(1)}, u32[]{:S(2)}, u32[]{:S(2)}) collective-permute-start(bf16[64,768]{1,0:T(8,128)(2,1)S(1)} %fusion.148), channel_id=1, source_target_pairs={{0,16},{8,24},{16,0},{24,8},{1,17},{9,25},{17,1},{25,9},{2,18},{10... | collective-permute-start | bytes 294920 | tf_op jit(solution)/shard_map/ppermute | solution.py:24
  60.2 6.2 %collective-permute-start.32 = (bf16[64,768]{1,0:T(8,128)(2,1)S(1)}, bf16[64,768]{1,0:T(8,128)(2,1)S(1)}, u32[]{:S(2)}, u32[]{:S(2)}) collective-permute-start(bf16[64,768]{1,0:T(8,128)(2,1)S(1)} %fusion.132), channel_id=1, source_target_pairs={{0,16},{8,24},{16,0},{24,8},{1,17},{9,25},{17,1},{25,9},{2,18},{10... | collective-permute-start | bytes 294920 | tf_op jit(solution)/shard_map/ppermute | solution.py:24
  61.2 6.1 %collective-permute-start.10 = (bf16[64,768]{1,0:T(8,128)(2,1)S(1)}, bf16[64,768]{1,0:T(8,128)(2,1)S(1)}, u32[]{:S(2)}, u32[]{:S(2)}) collective-permute-start(bf16[64,768]{1,0:T(8,128)(2,1)S(1)} %fusion.145), channel_id=1, source_target_pairs={{0,8},{8,0},{16,24},{24,16},{1,9},{9,1},{17,25},{25,17},{2,10},{10... | collective-permute-start | bytes 294920 | tf_op jit(solution)/shard_map/ppermute | solution.py:24
  62.1 7.4 %collective-permute-start.36 = (bf16[64,768]{1,0:T(8,128)(2,1)S(1)}, bf16[64,768]{1,0:T(8,128)(2,1)S(1)}, u32[]{:S(2)}, u32[]{:S(2)}) collective-permute-start(bf16[64,768]{1,0:T(8,128)(2,1)S(1)} %fusion.129), channel_id=1, source_target_pairs={{0,8},{8,0},{16,24},{24,16},{1,9},{9,1},{17,25},{25,17},{2,10},{10... | collective-permute-start | bytes 294920 | tf_op jit(solution)/shard_map/ppermute | solution.py:24
  63.4 7.2 %collective-permute-start.14 = (bf16[64,768]{1,0:T(8,128)(2,1)S(1)}, bf16[64,768]{1,0:T(8,128)(2,1)S(1)}, u32[]{:S(2)}, u32[]{:S(2)}) collective-permute-start(bf16[64,768]{1,0:T(8,128)(2,1)S(1)} %fusion.142), channel_id=1, source_target_pairs={{0,16},{8,24},{16,0},{24,8},{1,17},{9,25},{17,1},{25,9},{2,18},{10... | collective-permute-start | bytes 294920 | tf_op jit(solution)/shard_map/ppermute | solution.py:24
  64.6 8.6 %collective-permute-start.40 = (bf16[64,768]{1,0:T(8,128)(2,1)S(1)}, bf16[64,768]{1,0:T(8,128)(2,1)S(1)}, u32[]{:S(2)}, u32[]{:S(2)}) collective-permute-start(bf16[64,768]{1,0:T(8,128)(2,1)S(1)} %fusion.126), channel_id=1, source_target_pairs={{0,16},{8,24},{16,0},{24,8},{1,17},{9,25},{17,1},{25,9},{2,18},{10... | collective-permute-start | bytes 294920 | tf_op jit(solution)/shard_map/ppermute | solution.py:24
  65.5 27.9 %slice-start.4 = ((s8[9437184]{0:T(1024)(128)(4,1)}), s8[4194304]{0:T(1024)(128)(4,1)S(1)}, s32[]{:S(2)}) async-start(s8[9437184]{0:T(1024)(128)(4,1)} %bitcast.113), calls=%async_computation.5 | async-start | bytes 8388608
  66.4 6.8 %collective-permute-start.18 = (bf16[64,768]{1,0:T(8,128)(2,1)S(1)}, bf16[64,768]{1,0:T(8,128)(2,1)S(1)}, u32[]{:S(2)}, u32[]{:S(2)}) collective-permute-start(bf16[64,768]{1,0:T(8,128)(2,1)S(1)} %fusion.139), channel_id=1, source_target_pairs={{0,8},{8,0},{16,24},{24,16},{1,9},{9,1},{17,25},{25,17},{2,10},{10... | collective-permute-start | bytes 294920 | tf_op jit(solution)/shard_map/ppermute | solution.py:24
  67.3 8.9 %collective-permute-start.29 = (bf16[64,768]{1,0:T(8,128)(2,1)S(1)}, bf16[64,768]{1,0:T(8,128)(2,1)S(1)}, u32[]{:S(2)}, u32[]{:S(2)}) collective-permute-start(bf16[64,768]{1,0:T(8,128)(2,1)S(1)} %get-tuple-element.56), channel_id=1, source_target_pairs={{0,8},{8,0},{16,24},{24,16},{1,9},{9,1},{17,25},{25,17},{2,10},{10... | collective-permute-start | bytes 294920 | tf_op jit(solution)/shard_map/ppermute | solution.py:24
  69.5 7.4 %collective-permute-start.33 = (bf16[64,768]{1,0:T(8,128)(2,1)S(1)}, bf16[64,768]{1,0:T(8,128)(2,1)S(1)}, u32[]{:S(2)}, u32[]{:S(2)}) collective-permute-start(bf16[64,768]{1,0:T(8,128)(2,1)S(1)} %get-tuple-element.58), channel_id=1, source_target_pairs={{0,16},{8,24},{16,0},{24,8},{1,17},{9,25},{17,1},{25,9},{2,18},{10... | collective-permute-start | bytes 294920 | tf_op jit(solution)/shard_map/ppermute | solution.py:24
  71.7 6.2 %collective-permute-start.37 = (bf16[64,768]{1,0:T(8,128)(2,1)S(1)}, bf16[64,768]{1,0:T(8,128)(2,1)S(1)}, u32[]{:S(2)}, u32[]{:S(2)}) collective-permute-start(bf16[64,768]{1,0:T(8,128)(2,1)S(1)} %get-tuple-element.60), channel_id=1, source_target_pairs={{0,8},{8,0},{16,24},{24,16},{1,9},{9,1},{17,25},{25,17},{2,10},{10... | collective-permute-start | bytes 294920 | tf_op jit(solution)/shard_map/ppermute | solution.py:24
  74.2 5.7 %collective-permute-start.41 = (bf16[64,768]{1,0:T(8,128)(2,1)S(1)}, bf16[64,768]{1,0:T(8,128)(2,1)S(1)}, u32[]{:S(2)}, u32[]{:S(2)}) collective-permute-start(bf16[64,768]{1,0:T(8,128)(2,1)S(1)} %get-tuple-element.62), channel_id=1, source_target_pairs={{0,16},{8,24},{16,0},{24,8},{1,17},{9,25},{17,1},{25,9},{2,18},{10... | collective-permute-start | bytes 294920 | tf_op jit(solution)/shard_map/ppermute | solution.py:24
  74.5 7.5 %collective-permute-start.7 = (bf16[64,768]{1,0:T(8,128)(2,1)S(1)}, bf16[64,768]{1,0:T(8,128)(2,1)S(1)}, u32[]{:S(2)}, u32[]{:S(2)}) collective-permute-start(bf16[64,768]{1,0:T(8,128)(2,1)S(1)} %get-tuple-element.55), channel_id=1, source_target_pairs={{0,16},{8,24},{16,0},{24,8},{1,17},{9,25},{17,1},{25,9},{2,18},{10... | collective-permute-start | bytes 294920 | tf_op jit(solution)/shard_map/ppermute | solution.py:24
  76.2 6.2 %collective-permute-start.11 = (bf16[64,768]{1,0:T(8,128)(2,1)S(1)}, bf16[64,768]{1,0:T(8,128)(2,1)S(1)}, u32[]{:S(2)}, u32[]{:S(2)}) collective-permute-start(bf16[64,768]{1,0:T(8,128)(2,1)S(1)} %get-tuple-element.57), channel_id=1, source_target_pairs={{0,8},{8,0},{16,24},{24,16},{1,9},{9,1},{17,25},{25,17},{2,10},{10... | collective-permute-start | bytes 294920 | tf_op jit(solution)/shard_map/ppermute | solution.py:24
  76.9 7.2 %collective-permute-start.15 = (bf16[64,768]{1,0:T(8,128)(2,1)S(1)}, bf16[64,768]{1,0:T(8,128)(2,1)S(1)}, u32[]{:S(2)}, u32[]{:S(2)}) collective-permute-start(bf16[64,768]{1,0:T(8,128)(2,1)S(1)} %get-tuple-element.59), channel_id=1, source_target_pairs={{0,16},{8,24},{16,0},{24,8},{1,17},{9,25},{17,1},{25,9},{2,18},{10... | collective-permute-start | bytes 294920 | tf_op jit(solution)/shard_map/ppermute | solution.py:24
  77.9 6.6 %collective-permute-start.19 = (bf16[64,768]{1,0:T(8,128)(2,1)S(1)}, bf16[64,768]{1,0:T(8,128)(2,1)S(1)}, u32[]{:S(2)}, u32[]{:S(2)}) collective-permute-start(bf16[64,768]{1,0:T(8,128)(2,1)S(1)} %get-tuple-element.61), channel_id=1, source_target_pairs={{0,8},{8,0},{16,24},{24,16},{1,9},{9,1},{17,25},{25,17},{2,10},{10... | collective-permute-start | bytes 294920 | tf_op jit(solution)/shard_map/ppermute | solution.py:24
  79.9 15.9 %collective-permute-start.30 = (bf16[128,768]{1,0:T(8,128)(2,1)S(1)}, bf16[128,768]{1,0:T(8,128)(2,1)S(1)}, u32[]{:S(2)}, u32[]{:S(2)}) collective-permute-start(bf16[128,768]{1,0:T(8,128)(2,1)S(1)} %pad_maximum_fusion.11), channel_id=1, source_target_pairs={{0,16},{8,24},{16,0},{24,8},{1,17},{9,25},{17,1},{25,9},{2,18},{10... | collective-permute-start | bytes 589832 | tf_op jit(solution)/shard_map/ppermute | solution.py:24
  82.0 7.1 %collective-permute-start.34 = (bf16[128,768]{1,0:T(8,128)(2,1)S(1)}, bf16[128,768]{1,0:T(8,128)(2,1)S(1)}, u32[]{:S(2)}, u32[]{:S(2)}) collective-permute-start(bf16[128,768]{1,0:T(8,128)(2,1)S(1)} %pad_maximum_fusion.13), channel_id=1, source_target_pairs={{0,8},{8,0},{16,24},{24,16},{1,9},{9,1},{17,25},{25,17},{2,10},{10... | collective-permute-start | bytes 589832 | tf_op jit(solution)/shard_map/ppermute | solution.py:24
  82.5 10.1 %collective-permute-start.38 = (bf16[128,768]{1,0:T(8,128)(2,1)S(1)}, bf16[128,768]{1,0:T(8,128)(2,1)S(1)}, u32[]{:S(2)}, u32[]{:S(2)}) collective-permute-start(bf16[128,768]{1,0:T(8,128)(2,1)S(1)} %pad_maximum_fusion.14), channel_id=1, source_target_pairs={{0,16},{8,24},{16,0},{24,8},{1,17},{9,25},{17,1},{25,9},{2,18},{10... | collective-permute-start | bytes 589832 | tf_op jit(solution)/shard_map/ppermute | solution.py:24
  84.1 7.1 %collective-permute-start.42 = (bf16[128,768]{1,0:T(8,128)(2,1)S(1)}, bf16[128,768]{1,0:T(8,128)(2,1)S(1)}, u32[]{:S(2)}, u32[]{:S(2)}) collective-permute-start(bf16[128,768]{1,0:T(8,128)(2,1)S(1)} %pad_maximum_fusion.16), channel_id=1, source_target_pairs={{0,8},{8,0},{16,24},{24,16},{1,9},{9,1},{17,25},{25,17},{2,10},{10... | collective-permute-start | bytes 589832 | tf_op jit(solution)/shard_map/ppermute | solution.py:24
  84.5 13.0 %collective-permute-start.8 = (bf16[128,768]{1,0:T(8,128)(2,1)S(1)}, bf16[128,768]{1,0:T(8,128)(2,1)S(1)}, u32[]{:S(2)}, u32[]{:S(2)}) collective-permute-start(bf16[128,768]{1,0:T(8,128)(2,1)S(1)} %pad_maximum_fusion.5), channel_id=1, source_target_pairs={{0,8},{8,0},{16,24},{24,16},{1,9},{9,1},{17,25},{25,17},{2,10},{10... | collective-permute-start | bytes 589832 | tf_op jit(solution)/shard_map/ppermute | solution.py:24
  89.1 7.7 %collective-permute-start.12 = (bf16[128,768]{1,0:T(8,128)(2,1)S(1)}, bf16[128,768]{1,0:T(8,128)(2,1)S(1)}, u32[]{:S(2)}, u32[]{:S(2)}) collective-permute-start(bf16[128,768]{1,0:T(8,128)(2,1)S(1)} %pad_maximum_fusion.6), channel_id=1, source_target_pairs={{0,16},{8,24},{16,0},{24,8},{1,17},{9,25},{17,1},{25,9},{2,18},{10... | collective-permute-start | bytes 589832 | tf_op jit(solution)/shard_map/ppermute | solution.py:24
  91.2 6.4 %collective-permute-start.16 = (bf16[128,768]{1,0:T(8,128)(2,1)S(1)}, bf16[128,768]{1,0:T(8,128)(2,1)S(1)}, u32[]{:S(2)}, u32[]{:S(2)}) collective-permute-start(bf16[128,768]{1,0:T(8,128)(2,1)S(1)} %pad_maximum_fusion.8), channel_id=1, source_target_pairs={{0,8},{8,0},{16,24},{24,16},{1,9},{9,1},{17,25},{25,17},{2,10},{10... | collective-permute-start | bytes 589832 | tf_op jit(solution)/shard_map/ppermute | solution.py:24
  92.6 5.7 %collective-permute-start.20 = (bf16[128,768]{1,0:T(8,128)(2,1)S(1)}, bf16[128,768]{1,0:T(8,128)(2,1)S(1)}, u32[]{:S(2)}, u32[]{:S(2)}) collective-permute-start(bf16[128,768]{1,0:T(8,128)(2,1)S(1)} %pad_maximum_fusion.9), channel_id=1, source_target_pairs={{0,16},{8,24},{16,0},{24,8},{1,17},{9,25},{17,1},{25,9},{2,18},{10... | collective-permute-start | bytes 589832 | tf_op jit(solution)/shard_map/ppermute | solution.py:24
  96.7 4.3 %collective-permute-start.43 = (bf16[256,768]{1,0:T(8,128)(2,1)S(1)}, bf16[256,768]{1,0:T(8,128)(2,1)S(1)}, u32[]{:S(2)}, u32[]{:S(2)}) collective-permute-start(bf16[256,768]{1,0:T(8,128)(2,1)S(1)} %select_convert_fusion), channel_id=1, source_target_pairs={{0,1},{1,0},{2,3},{3,2},{4,5},{5,4},{6,7},{7,6},{8,9},{9,8},{10,11... | collective-permute-start | bytes 1179656 | tf_op jit(solution)/shard_map/ppermute | solution.py:27
  100.9 3.8 %collective-permute-start.21 = (bf16[256,768]{1,0:T(8,128)(2,1)S(1)}, bf16[256,768]{1,0:T(8,128)(2,1)S(1)}, u32[]{:S(2)}, u32[]{:S(2)}) collective-permute-start(bf16[256,768]{1,0:T(8,128)(2,1)S(1)} %select_convert_fusion.1), channel_id=1, source_target_pairs={{0,1},{1,0},{2,3},{3,2},{4,5},{5,4},{6,7},{7,6},{8,9},{9,8},{10,11... | collective-permute-start | bytes 1179656 | tf_op jit(solution)/shard_map/ppermute | solution.py:27
  101.1 5.7 %collective-permute-start.44 = (bf16[64,768]{1,0:T(8,128)(2,1)S(1)}, bf16[64,768]{1,0:T(8,128)(2,1)S(1)}, u32[]{:S(2)}, u32[]{:S(2)}) collective-permute-start(bf16[64,768]{1,0:T(8,128)(2,1)S(1)} %get-tuple-element.38), channel_id=1, source_target_pairs={{0,8},{8,0},{16,24},{24,16},{1,9},{9,1},{17,25},{25,17},{2,10},{10... | collective-permute-start | bytes 294920 | tf_op jit(solution)/shard_map/ppermute | solution.py:24
  101.8 6.6 %collective-permute-start.45 = (bf16[64,768]{1,0:T(8,128)(2,1)S(1)}, bf16[64,768]{1,0:T(8,128)(2,1)S(1)}, u32[]{:S(2)}, u32[]{:S(2)}) collective-permute-start(bf16[64,768]{1,0:T(8,128)(2,1)S(1)} %get-tuple-element.37), channel_id=1, source_target_pairs={{0,16},{8,24},{16,0},{24,8},{1,17},{9,25},{17,1},{25,9},{2,18},{10... | collective-permute-start | bytes 294920 | tf_op jit(solution)/shard_map/ppermute | solution.py:24
  102.9 6.6 %collective-permute-start.46 = (bf16[64,768]{1,0:T(8,128)(2,1)S(1)}, bf16[64,768]{1,0:T(8,128)(2,1)S(1)}, u32[]{:S(2)}, u32[]{:S(2)}) collective-permute-start(bf16[64,768]{1,0:T(8,128)(2,1)S(1)} %get-tuple-element.36), channel_id=1, source_target_pairs={{0,24},{8,16},{16,8},{24,0},{1,25},{9,17},{17,9},{25,1},{2,26},{10... | collective-permute-start | bytes 294920 | tf_op jit(solution)/shard_map/ppermute | solution.py:24
  104.8 17.7 %copy-start.1 = (bf16[128,768]{1,0:T(8,128)(2,1)S(1)}, bf16[128,768]{1,0:T(8,128)(2,1)}, u32[]{:S(2)}) copy-start(bf16[128,768]{1,0:T(8,128)(2,1)} %param.5) | copy-start | bytes 589828
  104.9 6.2 %collective-permute-start.22 = (bf16[64,768]{1,0:T(8,128)(2,1)S(1)}, bf16[64,768]{1,0:T(8,128)(2,1)S(1)}, u32[]{:S(2)}, u32[]{:S(2)}) collective-permute-start(bf16[64,768]{1,0:T(8,128)(2,1)S(1)} %get-tuple-element.28), channel_id=1, source_target_pairs={{0,8},{8,0},{16,24},{24,16},{1,9},{9,1},{17,25},{25,17},{2,10},{10... | collective-permute-start | bytes 294920 | tf_op jit(solution)/shard_map/ppermute | solution.py:24
  105.5 7.5 %collective-permute-start.23 = (bf16[64,768]{1,0:T(8,128)(2,1)S(1)}, bf16[64,768]{1,0:T(8,128)(2,1)S(1)}, u32[]{:S(2)}, u32[]{:S(2)}) collective-permute-start(bf16[64,768]{1,0:T(8,128)(2,1)S(1)} %get-tuple-element.27), channel_id=1, source_target_pairs={{0,16},{8,24},{16,0},{24,8},{1,17},{9,25},{17,1},{25,9},{2,18},{10... | collective-permute-start | bytes 294920 | tf_op jit(solution)/shard_map/ppermute | solution.py:24
  106.9 6.2 %collective-permute-start.24 = (bf16[64,768]{1,0:T(8,128)(2,1)S(1)}, bf16[64,768]{1,0:T(8,128)(2,1)S(1)}, u32[]{:S(2)}, u32[]{:S(2)}) collective-permute-start(bf16[64,768]{1,0:T(8,128)(2,1)S(1)} %get-tuple-element.26), channel_id=1, source_target_pairs={{0,24},{8,16},{16,8},{24,0},{1,25},{9,17},{17,9},{25,1},{2,26},{10... | collective-permute-start | bytes 294920 | tf_op jit(solution)/shard_map/ppermute | solution.py:24
  109.6 6.1 %collective-permute-start.47 = (bf16[128,768]{1,0:T(8,128)(2,1)S(1)}, bf16[128,768]{1,0:T(8,128)(2,1)S(1)}, u32[]{:S(2)}, u32[]{:S(2)}) collective-permute-start(bf16[128,768]{1,0:T(8,128)(2,1)S(1)} %pad_maximum_fusion.17), channel_id=1, source_target_pairs={{0,2},{1,3},{2,0},{3,1},{4,6},{5,7},{6,4},{7,5},{8,10},{9,11},{10,... | collective-permute-start | bytes 589832 | tf_op jit(solution)/shard_map/ppermute | solution.py:44
  113.2 7.8 %collective-permute-start.25 = (bf16[128,768]{1,0:T(8,128)(2,1)S(1)}, bf16[128,768]{1,0:T(8,128)(2,1)S(1)}, u32[]{:S(2)}, u32[]{:S(2)}) collective-permute-start(bf16[128,768]{1,0:T(8,128)(2,1)S(1)} %pad_maximum_fusion.10), channel_id=1, source_target_pairs={{0,2},{1,3},{2,0},{3,1},{4,6},{5,7},{6,4},{7,5},{8,10},{9,11},{10,... | collective-permute-start | bytes 589832 | tf_op jit(solution)/shard_map/ppermute | solution.py:44
  115.6 7.0 %collective-permute-start.48 = (bf16[64,768]{1,0:T(8,128)(2,1)S(1)}, bf16[64,768]{1,0:T(8,128)(2,1)S(1)}, u32[]{:S(2)}, u32[]{:S(2)}) collective-permute-start(bf16[64,768]{1,0:T(8,128)(2,1)S(1)} %fusion.152), channel_id=1, source_target_pairs={{0,4},{1,5},{2,6},{3,7},{4,0},{5,1},{6,2},{7,3},{8,12},{9,13},{10,... | collective-permute-start | bytes 294920 | tf_op jit(solution)/shard_map/ppermute | solution.py:44
  121.0 6.3 %collective-permute-start.26 = (bf16[64,768]{1,0:T(8,128)(2,1)S(1)}, bf16[64,768]{1,0:T(8,128)(2,1)S(1)}, u32[]{:S(2)}, u32[]{:S(2)}) collective-permute-start(bf16[64,768]{1,0:T(8,128)(2,1)S(1)} %fusion.154), channel_id=1, source_target_pairs={{0,4},{1,5},{2,6},{3,7},{4,0},{5,1},{6,2},{7,3},{8,12},{9,13},{10,... | collective-permute-start | bytes 294920 | tf_op jit(solution)/shard_map/ppermute | solution.py:44
